TPU v7x, 256 devices: a whole 4x4x8 slice. The times are simulated.
256 devices in a mesh: dp: 128 (over z, x, y_lo, core), tp: 2 (over y_hi).
Axes of the slice: x: 4, y: 4 (y_hi: 2, y_lo: 2; y = y_hi * 2 + y_lo), z: 8, core: 2. Of those that a mesh axis runs over, the one named last changes fastest.
Arguments:
- q_nope: bfloat16 [4096, 2048], P('dp', 'tp'), may hold values from -4 to 4
- q_rope: bfloat16 [4096, 1024], P('dp', 'tp'), may hold values from -80 to 80
- lengths: int32 [4096], P('dp'), may hold values from 1 to 512, as said below
- page_table: int32 [4096, 8], P('dp'), may hold values from 0 to 95, as said below
- lend_counts: int32 [4096, 2], P('dp'), may hold values from 0 to 2, as said below
- latent_pages: bfloat16 [12288, 64, 512], P('dp'), may hold values from -5 to 5
- rope_pages: bfloat16 [12288, 4096], P('dp'), may hold values from -4 to 4
- w_uk: bfloat16 [16, 128, 512], P('tp'), may hold values from -0.5 to 0.5
- w_uv: bfloat16 [16, 512, 128], P('tp'), may hold values from -0.75 to 0.75
- w_o: bfloat16 [2048, 2048], P('tp'), may hold values from -0.125 to 0.125
Outputs:
- attention_out: bfloat16 [4096, 2048], P('dp', 'tp')
Inputs may be any that keep to these rules, and one draw needn't show every extreme that they name: `lengths`: at least one live token in every request; some request reaches the most in every draw. For every request lend_counts[r, 0] + lend_counts[r, 1] is below its page count, so its first page is held by its own replica; every replica has a request that lends 2 pages each way. `page_table`: the 8 entries of a row are distinct. Entries for pages past a request's page count are not read.
All inputs are finite; a program needn't handle non-finite values.
Results may differ from a plain program's by a relative error of at most 0.012.
Values may be sent and summed in bfloat16 or wider, within the bound.
A program may use at most 128 MiB of HBM per device.

v0:
```python
from functools import reduce
import math

import jax
import jax.numpy as jnp
from jax import lax
from jax.sharding import PartitionSpec as P

ROPE = 64
NOPE = 128
PAGE = 64
MAXP = 8
LEND = 2


def from_behind(block, axis, distance):
    devices = range(lax.axis_size(axis))
    route = [((i - distance) % len(devices), i) for i in devices]
    return lax.ppermute(block, axis, route)


def in_blocks(x, dim, peers):
    before, after = (x.shape[:dim], x.shape[dim + 1 :])
    return jnp.moveaxis(x.reshape(*before, peers, -1, *after), dim, 0)


def sent_and_summed(x, axis, dim):
    blocks = in_blocks(x, dim, lax.axis_size(axis))
    arrived = lax.all_to_all(blocks, axis, split_axis=0, concat_axis=0, tiled=True)
    return arrived.astype(jnp.float32).sum(axis=0)


def gather_tokens(latent_pages, rope_pages, slot_ids):
    requests, pages_each = slot_ids.shape
    page_len = latent_pages.shape[1]
    latent = latent_pages[slot_ids].reshape(requests, pages_each * page_len, latent_pages.shape[2])
    rope_keys = rope_pages[slot_ids].reshape(requests, pages_each * page_len, ROPE)
    return (latent, rope_keys)


def plan_mask(plan_rows):
    filled = plan_rows[:, LEND:]
    offsets = jnp.arange(PAGE, dtype=jnp.int32)
    alive_mask = offsets[None, None, :] < filled[:, :, None]
    return alive_mask.reshape(plan_rows.shape[0], LEND * PAGE)


def attend(query_lat, query_rope, latent, rope_keys, alive_mask):
    score_scale = 1.0 / math.sqrt(NOPE + ROPE)
    scores = jnp.einsum("rhc,rtc->rht", query_lat, latent, preferred_element_type=jnp.float32)
    scores = (
        scores
        + jnp.einsum("rhe,rte->rht", query_rope, rope_keys, preferred_element_type=jnp.float32)
    ) * score_scale
    scores = jnp.where(alive_mask[:, None, :], scores, -jnp.inf)
    peak = jnp.maximum(jnp.max(scores, axis=-1), -1e30)
    weights = jnp.exp(scores - peak[..., None]).astype(jnp.bfloat16)
    total = jnp.sum(weights.astype(jnp.float32), axis=-1)
    summed = jnp.einsum("rht,rtc->rhc", weights, latent, preferred_element_type=jnp.float32)
    return (summed, peak, total)


def attend_pool(query_lat, query_rope, latent_pages, rope_pages, page_table, first_lent, lengths):
    score_scale = 1.0 / math.sqrt(NOPE + ROPE)
    requests, heads_here, _ = query_lat.shape
    slots = latent_pages.shape[0]
    pool_latent = latent_pages.reshape(slots * PAGE, latent_pages.shape[2])
    pool_rope = rope_pages.reshape(slots * PAGE, ROPE)
    page_ids = jnp.arange(MAXP, dtype=jnp.int32)
    slot_ids = jnp.arange(slots, dtype=jnp.int32)
    offsets = jnp.arange(PAGE, dtype=jnp.int32)
    matches = (page_table[:, :, None] == slot_ids[None, None, :]) & (
        page_ids[None, :, None] < first_lent[:, None, None]
    )
    live_token = page_ids[None, :, None] * PAGE + offsets[None, None, :] < lengths[:, None, None]
    own_mask = jnp.any(matches[:, :, :, None] & live_token[:, :, None, :], axis=1).reshape(
        requests, slots * PAGE
    )
    scores = jnp.einsum("rhc,tc->rht", query_lat, pool_latent, preferred_element_type=jnp.float32)
    scores = (
        scores
        + jnp.einsum("rhe,te->rht", query_rope, pool_rope, preferred_element_type=jnp.float32)
    ) * score_scale
    scores = jnp.where(own_mask[:, None, :], scores, -jnp.inf)
    peak = jnp.maximum(jnp.max(scores, axis=-1), -1e30)
    weights = jnp.exp(scores - peak[..., None]).astype(jnp.bfloat16)
    total = jnp.sum(weights.astype(jnp.float32), axis=-1)
    summed = jnp.einsum("rht,tc->rhc", weights, pool_latent, preferred_element_type=jnp.float32)
    return (summed, peak, total)


def combine_pieces(pieces):
    peak = reduce(jnp.maximum, [piece[1] for piece in pieces])
    factors = [jnp.exp(piece[1] - peak) for piece in pieces]
    numerator = reduce(
        jnp.add, [factor[..., None] * piece[0] for factor, piece in zip(factors, pieces)]
    )
    denominator = reduce(jnp.add, [factor * piece[2] for factor, piece in zip(factors, pieces)])
    return (numerator / denominator[..., None]).astype(jnp.bfloat16)


def shards(
    q_nope, q_rope, lengths, page_table, lend_counts, latent_pages, rope_pages, w_uk, w_uv, w_o
):
    requests = lengths.shape[0]
    heads_here = w_uk.shape[0]
    query_lat = jnp.einsum(
        "rhn,hnc->rhc",
        q_nope.reshape(requests, heads_here, NOPE),
        w_uk,
        preferred_element_type=jnp.float32,
    ).astype(jnp.bfloat16)
    query_rope = q_rope.reshape(requests, heads_here, ROPE)
    page_count = (lengths + PAGE - 1) // PAGE
    first_lent = page_count - lend_counts[:, 0] - lend_counts[:, 1]
    second = page_count - lend_counts[:, 1]

    def wanted(start_page, lent_count):
        step_ids = jnp.arange(LEND, dtype=jnp.int32)
        page_at = start_page[:, None] + step_ids[None, :]
        in_use = step_ids[None, :] < lent_count[:, None]
        slot_ids = jnp.take_along_axis(page_table, jnp.clip(page_at, 0, MAXP - 1), axis=1)
        filled = jnp.where(in_use, jnp.clip(lengths[:, None] - page_at * PAGE, 0, PAGE), 0)
        return jnp.concatenate([jnp.where(in_use, slot_ids, 0), filled], axis=1)

    ask_left = wanted(first_lent, lend_counts[:, 0])
    ask_right = wanted(second, lend_counts[:, 1])
    from_right = from_behind(ask_left, "dp", -1)
    from_left = from_behind(ask_right, "dp", 1)
    outgoing = (query_lat.reshape(requests, -1), q_rope)
    asked_next = from_behind((outgoing[0], outgoing[1]), "dp", -1)
    asked_prev = from_behind((outgoing[0], outgoing[1]), "dp", 1)

    def serve_rows(asked, plan_rows):
        latent, rope_keys = gather_tokens(latent_pages, rope_pages, plan_rows[:, :LEND])
        summed, peak, total = attend(
            asked[0].reshape(requests, heads_here, -1),
            asked[1].reshape(requests, heads_here, ROPE),
            latent,
            rope_keys,
            plan_mask(plan_rows),
        )
        return (summed.reshape(requests, -1), peak, total)

    back_left = from_behind(serve_rows(asked_next, from_right), "dp", 1)
    back_right = from_behind(serve_rows(asked_prev, from_left), "dp", -1)
    local_piece = attend_pool(
        query_lat, query_rope, latent_pages, rope_pages, page_table, first_lent, lengths
    )
    pieces = [
        local_piece,
        (back_left[0].reshape(requests, heads_here, -1), back_left[1], back_left[2]),
        (back_right[0].reshape(requests, heads_here, -1), back_right[1], back_right[2]),
    ]
    context = combine_pieces(pieces)
    head_outs = jnp.einsum(
        "rhc,hcv->rhv", context, w_uv, preferred_element_type=jnp.float32
    ).astype(jnp.bfloat16)
    head_outs = head_outs.reshape(requests, -1)
    partial_out = jnp.dot(head_outs, w_o, preferred_element_type=jnp.float32)
    return sent_and_summed(partial_out.astype(jnp.bfloat16), "tp", 1).astype(jnp.bfloat16)


def solution(mesh):
    in_specs = (
        P("dp", "tp"),
        P("dp", "tp"),
        P("dp"),
        P("dp", None),
        P("dp", None),
        P("dp", None, None),
        P("dp", None),
        P("tp", None, None),
        P("tp", None, None),
        P("tp", None),
    )
    out_specs = P("dp", "tp")
    return jax.shard_map(shards, mesh=mesh, in_specs=in_specs, out_specs=out_specs, check_vma=False)
```

profile of v0, /device:TPU:1, one launch (start us, length us, event | category | flops | bytes accessed | tf_op | source)
XLA Modules:
  0.0 114.0 jit_solution(4187235146235800946)
XLA Ops:
  0.0 2.7 %collective-permute-start.6 = (bf16[32,512]{1,0:T(8,128)(2,1)}, bf16[32,512]{1,0:T(8,128)(2,1)}, u32[]{:S(2)}, u32[]{:S(2)}) collective-permute-start(bf16[32,512]{1,0:T(8,128)(2,1)} %param.13), channel_id=1, source_target_pairs={{254,0},{0,2},{2,4},{4,6},{6,8},{8,10},{10,12},{12,14},{14,16},{16... | collective-permute-start | bytes 98312 | tf_op jit(solution)/shard_map/ppermute | solution.py:19
  2.7 0.5 collective-permute-start.2
  3.2 1.1 convolution_convert_fusion.1
  4.3 0.7 copy-done.6
  5.0 0.7 copy.98
  5.7 1.2 %collective-permute-start.5 = (bf16[32,4096]{1,0:T(8,128)(2,1)}, bf16[32,4096]{1,0:T(8,128)(2,1)}, u32[]{:S(2)}, u32[]{:S(2)}) collective-permute-start(bf16[32,4096]{1,0:T(8,128)(2,1)} %bitcast.20), channel_id=1, source_target_pairs={{254,0},{0,2},{2,4},{4,6},{6,8},{8,10},{10,12},{12,14},{14,16},{16... | collective-permute-start | bytes 786440 | tf_op jit(solution)/shard_map/ppermute | solution.py:19
  7.0 5.7 %collective-permute-start.1 = (bf16[32,4096]{1,0:T(8,128)(2,1)}, bf16[32,4096]{1,0:T(8,128)(2,1)}, u32[]{:S(2)}, u32[]{:S(2)}) collective-permute-start(bf16[32,4096]{1,0:T(8,128)(2,1)} %bitcast.20), channel_id=1, source_target_pairs={{2,0},{4,2},{6,4},{8,6},{10,8},{12,10},{14,12},{16,14},{18,16},{20... | collective-permute-start | bytes 786440 | tf_op jit(solution)/shard_map/ppermute | solution.py:19
  12.6 1.3 %slice_bitcast_fusion.1 = (s32[32]{0:T(128)}, s32[32]{0:T(128)S(1)}) fusion(s32[32,2]{0,1:T(2,128)} %param.16), kind=kLoop, calls=%fused_computation.89 | loop fusion | bytes 512 | tf_op jit(solution)/shard_map/squeeze | solution.py:115
  13.9 0.8 subtract_subtract_fusion
  14.7 0.7 fusion.25
  15.6 0.7 gather_fusion.5
  16.6 0.6 pad_add_fusion.1
  17.7 0.7 gather_fusion.4
  18.9 2.9 %and_reduce_fusion = pred[32,96,64]{1,2,0:T(8,128)(4,1)S(1)} fusion(pred[32,8,64]{2,1,0:T(8,128)(4,1)S(1)} %broadcast_compare_fusion, pred[32,8,96]{2,1,0:T(8,128)(4,1)S(1)} %fusion.16), kind=kLoop, calls=%fused_computation.6 | loop fusion | flops 2949120 | bytes 237568 | tf_op jit(solution)/shard_map/reduce_or | solution.py:76
  21.8 0.6 copy.74
  22.5 1.4 %broadcast_in_dim.40 = pred[32,6144]{1,0:T(8,128)(4,1)} reshape(pred[32,96,64]{2,1,0:T(8,128)(4,1)S(1)} %copy.74) | data formatting | bytes 393216 | tf_op jit(solution)/shard_map/jit(_where)/broadcast_in_dim | solution.py:84
  23.8 1.7 %reshape.175 = bf16[6144,64]{1,0:T(8,128)(2,1)S(1)} reshape(bf16[96,4096]{1,0:T(8,128)(2,1)S(1)} %copy-done.2) | data formatting | bytes 1572864 | tf_op jit(solution)/shard_map/reshape | solution.py:68
  25.6 4.8 %fusion.14 = f32[32,8,6144]{2,1,0:T(8,128)S(1)} fusion(bf16[6144,512,1]{1,0,2:T(8,128)(2,1)} %bitcast.99, bf16[32,8,512]{2,0,1:T(8,128)(2,1)} %bitcast.106), kind=kOutput, calls=%fused_computation.33 | convolution fusion | flops 1610612736 | bytes 12845056 | tf_op jit(solution)/shard_map/rhc,tc->rht/dot_general | solution.py:79
  30.4 4.6 %fusion.30 = (f32[32,8]{1,0:T(8,128)S(1)}, f32[32,8,6144]{2,1,0:T(8,128)}) fusion(f32[32,8,6144]{2,1,0:T(8,128)S(1)} %fusion.14, bf16[32,8,64]{2,1,0:T(8,128)(2,1)S(1)} %reshape.174, bf16[6144,64]{1,0:T(8,128)(2,1)S(1)} %reshape.175, pred[32,6144]{1,0:T(8,128)(4,1)S(1)} %copy-done.9), kind=kOutput, calls=%fused_computation.95 | convolution fusion | flops 207617792 | bytes 13599744 | tf_op jit(solution)/shard_map/rhe,te->rht/dot_general | solution.py:82
  35.1 6.2 %collective-permute-start = (s32[32,4]{0,1:T(4,128)S(1)}, s32[32,4]{0,1:T(4,128)S(1)}, u32[]{:S(2)}, u32[]{:S(2)}) collective-permute-start(s32[32,4]{0,1:T(4,128)S(1)} %pad_add_fusion), channel_id=1, source_target_pairs={{2,0},{4,2},{6,4},{8,6},{10,8},{12,10},{14,12},{16,14},{18,16},{20... | collective-permute-start | bytes 1544 | tf_op jit(solution)/shard_map/ppermute | solution.py:19
  41.2 0.8 fusion.27
  43.0 1.7 %gather_fusion.1 = bf16[64,4096]{1,0:T(8,128)(2,1)} fusion(bf16[96,4096]{1,0:T(8,128)(2,1)S(1)} %copy-done.2, s32[1024]{0:T(1024)S(1)} %pad_clamp_fusion.1), kind=kCustom, calls=%fused_computation.3 | custom fusion | bytes 1048832 | tf_op jit(solution)/shard_map/gather | solution.py:37
  44.7 5.7 %gather_fusion = bf16[64,64,512]{2,1,0:T(8,128)(2,1)} fusion(bf16[96,64,512]{2,1,0:T(8,128)(2,1)} %param.17, s32[1024]{0:T(1024)S(1)} %pad_clamp_fusion.1), kind=kCustom, calls=%fused_computation.2 | custom fusion | bytes 8388864 | tf_op jit(solution)/shard_map/gather | solution.py:36
  50.4 1.7 %gather_fusion.3 = bf16[64,4096]{1,0:T(8,128)(2,1)} fusion(bf16[96,4096]{1,0:T(8,128)(2,1)S(1)} %copy-done.2, s32[1024]{0:T(1024)S(1)} %pad_clamp_fusion), kind=kCustom, calls=%fused_computation.5 | custom fusion | bytes 1048832 | tf_op jit(solution)/shard_map/gather | solution.py:37
  52.0 5.7 %gather_fusion.2 = bf16[64,64,512]{2,1,0:T(8,128)(2,1)} fusion(bf16[96,64,512]{2,1,0:T(8,128)(2,1)} %param.17, s32[1024]{0:T(1024)S(1)} %pad_clamp_fusion), kind=kCustom, calls=%fused_computation.4 | custom fusion | bytes 8388864 | tf_op jit(solution)/shard_map/gather | solution.py:36
  57.8 1.1 reshape.183
  58.9 2.1 %reshape.179 = bf16[32,128,64]{2,1,0:T(8,128)(2,1)S(1)} reshape(bf16[64,4096]{1,0:T(8,128)(2,1)} %gather_fusion.1) | data formatting | bytes 1048576 | tf_op jit(solution)/shard_map/reshape | solution.py:37
  61.0 0.9 reshape.184
  61.8 0.6 convolution_bitcast_fusion
  62.6 0.6 convolution_bitcast_fusion.1
  63.2 1.4 %copy.100 = bf16[4,8,8,512]{3,2,1,0:T(8,128)(2,1)S(1)} copy(bf16[4,8,8,512]{3,1,2,0:T(8,128)(2,1)} %bitcast.24) | data formatting | bytes 524288
  64.6 3.6 %fusion.29 = (f32[32,8]{1,0:T(8,128)S(1)}, f32[32,8,128]{2,1,0:T(8,128)S(1)}) fusion(f32[32,8,128]{2,1,0:T(8,128)S(1)} %convolution_bitcast_fusion.1, bf16[32,8,512]{2,1,0:T(8,128)(2,1)S(1)} %bitcast.110, bf16[32,128,512]{2,1,0:T(8,128)(2,1)} %bitcast.97, pred[32,128]{1,0:T(8,128)(4,1)S(1)} %get-tuple-element.22), kind=kOutput, calls=%fused_computation.94 | convolution fusion | flops 33685248 | bytes 4723712 | tf_op jit(solution)/shard_map/rhc,rtc->rht/dot_general | solution.py:50
  68.5 0.7 fusion.21
  69.2 1.4 %copy.101 = bf16[4,8,8,512]{3,2,1,0:T(8,128)(2,1)S(1)} copy(bf16[4,8,8,512]{3,1,2,0:T(8,128)(2,1)} %bitcast.27) | data formatting | bytes 524288
  70.7 1.3 %fusion.28 = (f32[32,8]{1,0:T(8,128)S(1)}, f32[32,8,128]{2,1,0:T(8,128)S(1)}) fusion(f32[32,8,128]{2,1,0:T(8,128)S(1)} %convolution_bitcast_fusion, bf16[32,8,512]{2,1,0:T(8,128)(2,1)S(1)} %bitcast.109, bf16[32,128,512]{2,1,0:T(8,128)(2,1)S(1)} %bitcast.95, pred[32,128]{1,0:T(8,128)(4,1)S(1)} %get-tuple-element.23), kind=kOutput, calls=%fused_computation.93 | convolution fusion | flops 33685248 | bytes 4723712 | tf_op jit(solution)/shard_map/rhc,rtc->rht/dot_general | solution.py:50
  72.0 0.7 fusion.22
  72.9 6.5 %collective-permute-start.7 = (f32[32,8]{1,0:T(8,128)S(1)}, f32[32,8]{1,0:T(8,128)S(1)}, u32[]{:S(2)}, u32[]{:S(2)}) collective-permute-start(f32[32,8]{1,0:T(8,128)S(1)} %broadcast_maximum_fusion), channel_id=1, source_target_pairs={{2,0},{4,2},{6,4},{8,6},{10,8},{12,10},{14,12},{16,14},{18,16},{20... | collective-permute-start | bytes 3080 | tf_op jit(solution)/shard_map/ppermute | solution.py:19
  79.8 0.3 copy.104
  80.1 6.0 %collective-permute-start.11 = (f32[32,8]{1,0:T(8,128)S(1)}, f32[32,8]{1,0:T(8,128)S(1)}, u32[]{:S(2)}, u32[]{:S(2)}) collective-permute-start(f32[32,8]{1,0:T(8,128)S(1)} %convert_reduce_fusion.1), channel_id=1, source_target_pairs={{2,0},{4,2},{6,4},{8,6},{10,8},{12,10},{14,12},{16,14},{18,16},{20... | collective-permute-start | bytes 3080 | tf_op jit(solution)/shard_map/ppermute | solution.py:19
  86.2 5.9 %collective-permute-start.9 = (f32[32,4096]{1,0:T(8,128)S(1)}, f32[32,4096]{1,0:T(8,128)S(1)}, u32[]{:S(2)}, u32[]{:S(2)}) collective-permute-start(f32[32,4096]{1,0:T(8,128)S(1)} %bitcast.114), channel_id=1, source_target_pairs={{2,0},{4,2},{6,4},{8,6},{10,8},{12,10},{14,12},{16,14},{18,16},{20... | collective-permute-start | bytes 1572872 | tf_op jit(solution)/shard_map/ppermute | solution.py:19
  92.1 1.0 convert_reduce_fusion
  93.2 0.3 copy.103
  93.5 7.6 %collective-permute-done.9 = f32[32,4096]{1,0:T(8,128)S(1)} collective-permute-done((f32[32,4096]{1,0:T(8,128)S(1)}, f32[32,4096]{1,0:T(8,128)S(1)}, u32[]{:S(2)}, u32[]{:S(2)}) %collective-permute-start.9) | collective-permute-done | bytes 524320 | tf_op jit(solution)/shard_map/ppermute | solution.py:19
  101.5 1.9 %fusion.11 = bf16[32,8,512]{2,1,0:T(8,128)(2,1)S(1)} fusion(f32[4,8,8,512]{3,2,1,0:T(8,128)S(1)} %copy.105, f32[4,8,8,512]{3,2,1,0:T(8,128)S(1)} %copy.103, f32[32,8]{1,0:T(8,128)S(1)} %get-tuple-element.6, f32[32,8]{1,0:T(8,128)S(1)} %get-tuple-element.9, f32[32,8]{1,0:T(8,128)S(1)} %get-tuple-element.8, f32[32,8]{1,0:T(8,128)S(1)} %get-tuple-element.7, ...), kind=kOutput, calls=%fused_computation.29 | convolution fusion | flops 1614675968 | bytes 13898752 | tf_op jit(solution)/shard_map/rht,tc->rhc/dot_general | solution.py:88
  103.4 0.3 fusion.7
  104.0 0.8 convolution_convert_fusion
  104.8 8.5 %all_to_all.5 = bf16[2,32,1024]{2,1,0:T(8,128)(2,1)S(1)} all-to-all(bf16[2,32,1024]{2,1,0:T(8,128)(2,1)S(1)} %bitcast.116), channel_id=1, replica_groups=mesh['dp'=128,'tp'=2] {'tp'}, dimensions={0} | all-to-all | bytes 262144 | tf_op jit(solution)/shard_map/all_to_all | solution.py:29
  113.3 0.7 reduce_sum.42
  (102 shorter events, 4.2 us)
Async XLA Ops:
  0.0 3.2 %copy-start = (bf16[8,128,512]{2,1,0:T(8,128)(2,1)S(1)}, bf16[8,128,512]{2,1,0:T(8,128)(2,1)}, u32[]{:S(2)}) copy-start(bf16[8,128,512]{2,1,0:T(8,128)(2,1)} %param.19) | copy-start | bytes 3145732
  0.0 15.6 %copy-start.1 = (s32[32,8]{0,1:T(8,128)S(1)}, s32[32,8]{0,1:T(8,128)}, u32[]{:S(2)}) copy-start(s32[32,8]{0,1:T(8,128)} %param.15) | copy-start | bytes 3076
  0.0 61.0 %collective-permute-start.6 = (bf16[32,512]{1,0:T(8,128)(2,1)}, bf16[32,512]{1,0:T(8,128)(2,1)}, u32[]{:S(2)}, u32[]{:S(2)}) collective-permute-start(bf16[32,512]{1,0:T(8,128)(2,1)} %param.13), channel_id=1, source_target_pairs={{254,0},{0,2},{2,4},{4,6},{6,8},{8,10},{10,12},{12,14},{14,16},{16... | collective-permute-start | bytes 98312 | tf_op jit(solution)/shard_map/ppermute | solution.py:19
  2.7 59.8 %collective-permute-start.2 = (bf16[32,512]{1,0:T(8,128)(2,1)}, bf16[32,512]{1,0:T(8,128)(2,1)S(1)}, u32[]{:S(2)}, u32[]{:S(2)}) collective-permute-start(bf16[32,512]{1,0:T(8,128)(2,1)} %param.13), channel_id=1, source_target_pairs={{2,0},{4,2},{6,4},{8,6},{10,8},{12,10},{14,12},{16,14},{18,16},{20... | collective-permute-start | bytes 98312 | tf_op jit(solution)/shard_map/ppermute | solution.py:19
  4.3 0.7 copy-start.6
  5.7 63.5 %collective-permute-start.5 = (bf16[32,4096]{1,0:T(8,128)(2,1)}, bf16[32,4096]{1,0:T(8,128)(2,1)}, u32[]{:S(2)}, u32[]{:S(2)}) collective-permute-start(bf16[32,4096]{1,0:T(8,128)(2,1)} %bitcast.20), channel_id=1, source_target_pairs={{254,0},{0,2},{2,4},{4,6},{6,8},{8,10},{10,12},{12,14},{14,16},{16... | collective-permute-start | bytes 786440 | tf_op jit(solution)/shard_map/ppermute | solution.py:19
  7.0 56.3 %collective-permute-start.1 = (bf16[32,4096]{1,0:T(8,128)(2,1)}, bf16[32,4096]{1,0:T(8,128)(2,1)}, u32[]{:S(2)}, u32[]{:S(2)}) collective-permute-start(bf16[32,4096]{1,0:T(8,128)(2,1)} %bitcast.20), channel_id=1, source_target_pairs={{2,0},{4,2},{6,4},{8,6},{10,8},{12,10},{14,12},{16,14},{18,16},{20... | collective-permute-start | bytes 786440 | tf_op jit(solution)/shard_map/ppermute | solution.py:19
  14.7 2.5 %copy-start.13 = (s32[32]{0:T(128)}, s32[32]{0:T(128)S(1)}, u32[]{:S(2)}) copy-start(s32[32]{0:T(128)S(1)} %get-tuple-element.10) | copy-start | bytes 388
  15.6 0.9 copy-start.11
  15.6 1.7 %copy-start.10 = (bf16[32,512]{1,0:T(8,128)(2,1)S(1)}, bf16[32,512]{1,0:T(8,128)(2,1)}, u32[]{:S(2)}) copy-start(bf16[32,512]{1,0:T(8,128)(2,1)} %param.13) | copy-start | bytes 98308
  17.2 17.9 %collective-permute-start.4 = (s32[32,4]{0,1:T(4,128)}, s32[32,4]{0,1:T(4,128)}, u32[]{:S(2)}, u32[]{:S(2)}) collective-permute-start(s32[32,4]{0,1:T(4,128)} %pad_add_fusion.1), channel_id=1, source_target_pairs={{254,0},{0,2},{2,4},{4,6},{6,8},{8,10},{10,12},{12,14},{14,16},{16... | collective-permute-start | bytes 1544 | tf_op jit(solution)/shard_map/ppermute | solution.py:19
  17.7 6.1 %copy-start.2 = (bf16[96,4096]{1,0:T(8,128)(2,1)S(1)}, bf16[96,4096]{1,0:T(8,128)(2,1)}, u32[]{:S(2)}) copy-start(bf16[96,4096]{1,0:T(8,128)(2,1)} %param.18) | copy-start | bytes 2359300
  25.5 4.8 %copy-start.9 = (pred[32,6144]{1,0:T(8,128)(4,1)S(1)}, pred[32,6144]{1,0:T(8,128)(4,1)}, u32[]{:S(2)}) copy-start(pred[32,6144]{1,0:T(8,128)(4,1)} %broadcast_in_dim.40) | copy-start | bytes 589828
  30.3 4.6 %copy-start.12 = (s32[32]{0:T(128)S(1)}, s32[32]{0:T(128)}, u32[]{:S(2)}) copy-start(s32[32]{0:T(128)} %param.14) | copy-start | bytes 388
  30.4 4.6 %copy-start.14 = (s32[32]{0:T(128)S(1)}, s32[32]{0:T(128)}, u32[]{:S(2)}) copy-start(s32[32]{0:T(128)} %copy-done.13) | copy-start | bytes 388
  30.4 4.6 %copy-start.15 = (s32[32]{0:T(128)S(1)}, s32[32]{0:T(128)}, u32[]{:S(2)}) copy-start(s32[32]{0:T(128)} %get-tuple-element.18) | copy-start | bytes 388
  35.1 7.0 %collective-permute-start = (s32[32,4]{0,1:T(4,128)S(1)}, s32[32,4]{0,1:T(4,128)S(1)}, u32[]{:S(2)}, u32[]{:S(2)}) collective-permute-start(s32[32,4]{0,1:T(4,128)S(1)} %pad_add_fusion), channel_id=1, source_target_pairs={{2,0},{4,2},{6,4},{8,6},{10,8},{12,10},{14,12},{16,14},{18,16},{20... | collective-permute-start | bytes 1544 | tf_op jit(solution)/shard_map/ppermute | solution.py:19
  52.0 5.7 %copy-start.7 = (bf16[64,4096]{1,0:T(8,128)(2,1)S(1)}, bf16[64,4096]{1,0:T(8,128)(2,1)}, u32[]{:S(2)}) copy-start(bf16[64,4096]{1,0:T(8,128)(2,1)} %gather_fusion.3) | copy-start | bytes 1572868
  62.6 5.9 %copy-start.4 = (bf16[64,64,512]{2,1,0:T(8,128)(2,1)S(1)}, bf16[64,64,512]{2,1,0:T(8,128)(2,1)}, u32[]{:S(2)}) copy-start(bf16[64,64,512]{2,1,0:T(8,128)(2,1)} %gather_fusion) | copy-start | bytes 12582916
  64.6 6.1 %copy-start.3 = (bf16[64,64,512]{2,1,0:T(8,128)(2,1)S(1)}, bf16[64,64,512]{2,1,0:T(8,128)(2,1)}, u32[]{:S(2)}) copy-start(bf16[64,64,512]{2,1,0:T(8,128)(2,1)} %gather_fusion.2) | copy-start | bytes 12582916
  68.3 24.9 %collective-permute-start.3 = (f32[32,8]{1,0:T(8,128)S(1)}, f32[32,8]{1,0:T(8,128)S(1)}, u32[]{:S(2)}, u32[]{:S(2)}) collective-permute-start(f32[32,8]{1,0:T(8,128)S(1)} %broadcast_maximum_fusion.1), channel_id=1, source_target_pairs={{254,0},{0,2},{2,4},{4,6},{6,8},{8,10},{10,12},{12,14},{14,16},{16... | collective-permute-start | bytes 3080 | tf_op jit(solution)/shard_map/ppermute | solution.py:19
  68.5 23.6 %slice-start.2 = ((s8[6291456]{0:T(1024)(128)(4,1)}), s8[4194304]{0:T(1024)(128)(4,1)S(1)}, s32[]{:S(2)}) async-start(s8[6291456]{0:T(1024)(128)(4,1)} %bitcast.103), calls=%async_computation.3 | async-start | bytes 8388608
  70.6 15.5 %collective-permute-start.10 = (f32[32,8]{1,0:T(8,128)S(1)}, f32[32,8]{1,0:T(8,128)S(1)}, u32[]{:S(2)}, u32[]{:S(2)}) collective-permute-start(f32[32,8]{1,0:T(8,128)S(1)} %convert_reduce_fusion.2), channel_id=1, source_target_pairs={{254,0},{0,2},{2,4},{4,6},{6,8},{8,10},{10,12},{12,14},{14,16},{16... | collective-permute-start | bytes 3080 | tf_op jit(solution)/shard_map/ppermute | solution.py:19
  70.7 21.4 %slice-start.3 = ((s8[6291456]{0:T(1024)(128)(4,1)}), s8[2097152]{0:T(1024)(128)(4,1)S(1)}, s32[]{:S(2)}) async-start(s8[6291456]{0:T(1024)(128)(4,1)} %bitcast.103), calls=%async_computation.4 | async-start | bytes 4194304
  72.0 29.4 %slice-start = ((s8[6291456]{0:T(1024)(128)(4,1)}), s8[4194304]{0:T(1024)(128)(4,1)S(1)}, s32[]{:S(2)}) async-start(s8[6291456]{0:T(1024)(128)(4,1)} %bitcast.100), calls=%async_computation.1 | async-start | bytes 8388608
  72.9 20.2 %collective-permute-start.7 = (f32[32,8]{1,0:T(8,128)S(1)}, f32[32,8]{1,0:T(8,128)S(1)}, u32[]{:S(2)}, u32[]{:S(2)}) collective-permute-start(f32[32,8]{1,0:T(8,128)S(1)} %broadcast_maximum_fusion), channel_id=1, source_target_pairs={{2,0},{4,2},{6,4},{8,6},{10,8},{12,10},{14,12},{16,14},{18,16},{20... | collective-permute-start | bytes 3080 | tf_op jit(solution)/shard_map/ppermute | solution.py:19
  79.7 13.4 %collective-permute-start.8 = (f32[32,4096]{1,0:T(8,128)S(1)}, f32[32,4096]{1,0:T(8,128)S(1)}, u32[]{:S(2)}, u32[]{:S(2)}) collective-permute-start(f32[32,4096]{1,0:T(8,128)S(1)} %bitcast.112), channel_id=1, source_target_pairs={{254,0},{0,2},{2,4},{4,6},{6,8},{8,10},{10,12},{12,14},{14,16},{16... | collective-permute-start | bytes 1572872 | tf_op jit(solution)/shard_map/ppermute | solution.py:19
  80.1 13.0 %collective-permute-start.11 = (f32[32,8]{1,0:T(8,128)S(1)}, f32[32,8]{1,0:T(8,128)S(1)}, u32[]{:S(2)}, u32[]{:S(2)}) collective-permute-start(f32[32,8]{1,0:T(8,128)S(1)} %convert_reduce_fusion.1), channel_id=1, source_target_pairs={{2,0},{4,2},{6,4},{8,6},{10,8},{12,10},{14,12},{16,14},{18,16},{20... | collective-permute-start | bytes 3080 | tf_op jit(solution)/shard_map/ppermute | solution.py:19
  86.2 14.9 %collective-permute-start.9 = (f32[32,4096]{1,0:T(8,128)S(1)}, f32[32,4096]{1,0:T(8,128)S(1)}, u32[]{:S(2)}, u32[]{:S(2)}) collective-permute-start(f32[32,4096]{1,0:T(8,128)S(1)} %bitcast.114), channel_id=1, source_target_pairs={{2,0},{4,2},{6,4},{8,6},{10,8},{12,10},{14,12},{16,14},{18,16},{20... | collective-permute-start | bytes 1572872 | tf_op jit(solution)/shard_map/ppermute | solution.py:19
  92.1 9.3 %slice-start.1 = ((s8[6291456]{0:T(1024)(128)(4,1)}), s8[2097152]{0:T(1024)(128)(4,1)S(1)}, s32[]{:S(2)}) async-start(s8[6291456]{0:T(1024)(128)(4,1)} %bitcast.100), calls=%async_computation.2 | async-start | bytes 4194304
  101.4 1.9 %copy-start.8 = (bf16[8,512,128]{2,1,0:T(8,128)(2,1)S(1)}, bf16[8,512,128]{2,1,0:T(8,128)(2,1)}, u32[]{:S(2)}) copy-start(bf16[8,512,128]{2,1,0:T(8,128)(2,1)} %param.20) | copy-start | bytes 3145732
  101.4 2.5 %copy-start.5 = (bf16[1024,2048]{1,0:T(8,128)(2,1)S(1)}, bf16[1024,2048]{1,0:T(8,128)(2,1)}, u32[]{:S(2)}) copy-start(bf16[1024,2048]{1,0:T(8,128)(2,1)} %param.21) | copy-start | bytes 12582916
where the time goes:
time: 114 us
  starting transfers between devices  34.9 us (31%)
  local copies, waits for them, and re-layouts  33.1 us (29%)
  matrix products  21 us (18%)
  blocking collectives  8.51 us (7%)
  other arithmetic  8.27 us (7%)
  waiting for transfers between devices  7.62 us (7%)
    ppermute x12, starting transfers between devices, from_behind(): return lax.ppermute(block, axis, route)  34.9 us
    gather x2, local copies, waits for them, and re-layouts, gather_tokens(): latent_pages[slot_ids]  11.4 us
    all_to_all x1, blocking collectives, sent_and_summed(): lax.all_to_all(blocks, axis, split_axis=0, concat_axis=0, tiled=True)  8.51 us
    ppermute x12, waiting for transfers between devices, from_behind(): return lax.ppermute(block, axis, route)  7.62 us
    unnamed x47, local copies, waits for them, and re-layouts  5.16 us
    dot_general x2, matrix products, attend(): jnp.einsum('rhc,rtc->rht', query_lat, latent, preferred_element_type=jnp....  4.86 us
    dot_general x1, matrix products, attend_pool(): jnp.einsum('rhc,tc->rht', query_lat, pool_latent, preferred_element_type=...  4.77 us
    dot_general x1, matrix products, attend_pool(): jnp.einsum('rhe,te->rht', query_rope, pool_rope, preferred_element_type=j...  4.56 us
  transfers between devices with their start and end apart: 12, of which 1 were waited for; matrix products, arithmetic and copies ran while one was open for 50% of the time, Pallas kernels for 0%

commit v1 on v0

v1 whole, which is shorter than its diff:
```python
import functools
import math

import jax
import jax.numpy as jnp
from jax import lax
from jax.experimental import pallas as pl
from jax.experimental.pallas import tpu as pltpu
from jax.sharding import PartitionSpec as P

ROPE = 64
NOPE = 128
VDIM = 128
PAGE = 64
MAXP = 8
LEND = 2
MESH = pl.DeviceIdType.MESH
NEG = -3e38
SCALE2 = math.log2(math.e) / math.sqrt(NOPE + ROPE)
COL_A, COL_B, COL_LEN = 8, 9, 10
CHUNK_PAGES = 16
F32 = jnp.float32
BF16 = jnp.bfloat16


def dot(a, b):
    return lax.dot_general(a, b, (((1,), (0,)), ((), ())), preferred_element_type=F32)


def dot_t(a, b):
    return lax.dot_general(a, b, (((1,), (1,)), ((), ())), preferred_element_type=F32)


def iota(shape, dim):
    return lax.broadcasted_iota(jnp.int32, shape, dim)


def doubled_rope(q_rope, head):
    pair = q_rope[:, (head // 2) * 128 : (head // 2 + 1) * 128].astype(F32)
    turned = pltpu.roll(pair, 64, 1)
    low = iota(pair.shape, 1) < 64
    return jnp.where(low, pair, turned) if head % 2 == 0 else jnp.where(low, turned, pair)


def kernel(
    n_dp,
    qn_hbm, qr_hbm, tab_hbm, lat_hbm, rope_hbm, wuk_hbm, wuv_hbm, wo_hbm,
    out_ref,
    qn, qr, tab, plan, lat, rope, wuk, wuv, wo,
    qn_in, qr_in, tab_in, tab_sm,
    perm, keys, q_own, bias, scores, probs, acc,
    q_far, s_far, o_far, m_far, l_far,
    u_out, ml_out, u_in, ml_in, heads_out, y_out, y_in,
    load_sem, lat_sem, sm_sem, qsend_sem, qrecv_sem, usend_sem, urecv_sem, ysend_sem, yrecv_sem,
):
    reqs = qn.shape[0]
    n_heads = wuk.shape[0]
    slots = rope.shape[0]
    latent = lat.shape[2]
    half = wo.shape[2]
    rows = reqs * n_heads
    chunk = CHUNK_PAGES * PAGE

    me = lax.axis_index("dp")
    side = lax.axis_index("tp")
    nxt = lax.rem(me + 1, n_dp)
    prv = lax.rem(me + n_dp - 1, n_dp)

    def local(src, dst, i):
        copy = pltpu.make_async_copy(src, dst, load_sem.at[i])
        copy.start()
        return copy

    c_qn = local(qn_hbm, qn, 0)
    c_qr = local(qr_hbm, qr, 1)
    c_tab = local(tab_hbm, tab, 2)
    c_wuk = local(wuk_hbm, wuk, 3)
    c_rope = local(rope_hbm, rope, 4)
    c_lat = []
    for i in range(slots // CHUNK_PAGES):
        part = pl.ds(i * CHUNK_PAGES, CHUNK_PAGES)
        copy = pltpu.make_async_copy(lat_hbm.at[part], lat.at[part], lat_sem.at[i])
        copy.start()
        c_lat.append(copy)
    c_wuv = local(wuv_hbm, wuv, 5)
    c_wo0 = local(wo_hbm.at[:, pl.ds((1 - side) * half, half)], wo.at[0], 6)
    c_wo1 = local(wo_hbm.at[:, pl.ds(side * half, half)], wo.at[1], 7)

    barrier = pltpu.get_barrier_semaphore()
    pl.semaphore_signal(barrier, inc=1, device_id={"dp": prv}, device_id_type=MESH)
    pl.semaphore_signal(barrier, inc=1, device_id={"dp": nxt}, device_id_type=MESH)
    pl.semaphore_signal(barrier, inc=1, device_id={"tp": 1 - side}, device_id_type=MESH)
    pl.semaphore_wait(barrier, 3)

    def ask(d, i, src, dst):
        copy = pltpu.make_async_remote_copy(
            src_ref=src, dst_ref=dst.at[d],
            send_sem=qsend_sem.at[d, i], recv_sem=qrecv_sem.at[d, i],
            device_id={"dp": prv if d == 0 else nxt}, device_id_type=MESH,
        )
        copy.start()
        return copy

    c_qn.wait()
    c_qr.wait()
    asks = [[ask(d, 0, qn, qn_in), ask(d, 1, qr, qr_in)] for d in range(2)]
    c_tab.wait()

    lane = iota((reqs, 128), 1)

    def column(i):
        return jnp.broadcast_to(tab[:, i : i + 1], (reqs, 128))

    table = [column(k) for k in range(MAXP)]
    length = column(COL_LEN)
    n_pages = (length + (PAGE - 1)) >> 6
    first = n_pages - column(COL_A) - column(COL_B)
    for d in range(2):
        start = first if d == 0 else n_pages - column(COL_B)
        held = column(COL_A + d)
        packed = jnp.zeros((reqs, 128), jnp.int32)
        for j in range(LEND):
            at = start + j
            slot = jnp.zeros((reqs, 128), jnp.int32)
            for k in range(MAXP):
                slot = jnp.where(at == k, table[k], slot)
            used = held > j
            slot = jnp.where(used, jnp.clip(slot, 0, slots - 1), 0)
            live = jnp.where(used, jnp.clip(length - at * PAGE, 0, PAGE), 0)
            packed = jnp.where(lane == j, slot, packed)
            packed = jnp.where(lane == LEND + j, live, packed)
        plan[d] = packed
    for d in range(2):
        asks[d].append(ask(d, 2, plan.at[d], tab_in))

    out_row = iota((512, 256), 0)
    in_row = iota((512, 256), 1)
    hit = ((out_row >> 5) == (in_row & 15)) & (((out_row & 31) >> 1) == (in_row >> 4))
    perm[...] = jnp.where(hit, 1.0, 0.0).astype(BF16)

    count = jnp.zeros((reqs, 128), jnp.int32)
    for k in range(MAXP):
        live = jnp.clip(length - k * PAGE, 0, PAGE)
        count = count + jnp.where((lane == table[k]) & (first > k), live, 0)
    for g in range(slots // 2):
        even = jnp.broadcast_to(count[:, 2 * g : 2 * g + 1], (reqs, 128))
        odd = jnp.broadcast_to(count[:, 2 * g + 1 : 2 * g + 2], (reqs, 128))
        limit = jnp.where(lane < 64, even, odd)
        bias[:, g * 128 : (g + 1) * 128] = jnp.where((lane & 63) < limit, 0.0, NEG)

    c_wuk.wait()
    for h in range(n_heads):
        mine = pl.ds(h * reqs, reqs)
        q_own[mine, 0:latent] = dot(qn[:, h * NOPE : (h + 1) * NOPE], wuk[h]).astype(BF16)
        q_own[mine, latent : latent + 128] = doubled_rope(qr, h).astype(BF16)

    c_rope.wait()
    row_odd = (iota((512, 128), 0) & 1) == 1
    lane_high = iota((512, 128), 1) >= 64
    keep = row_odd == lane_high
    for g in range(slots // 16):
        page_rows = pl.ds(g * 16, 16)
        left = jnp.concatenate(
            [rope[page_rows, j * 128 : (j + 1) * 128] for j in range(16)], axis=0
        )
        right = jnp.concatenate(
            [rope[page_rows, (16 + j) * 128 : (17 + j) * 128] for j in range(16)], axis=0
        )
        moved = dot(perm[...], jnp.concatenate([left, right], axis=1))
        for s in range(2):
            part = jnp.where(keep, moved[:, s * 128 : (s + 1) * 128], 0.0).astype(BF16)
            keys[page_rows, s * 32 : (s + 1) * 32, :] = part.reshape(16, 32, 128)

    top = None
    for i in range(slots // CHUNK_PAGES):
        c_lat[i].wait()
        for j in range(CHUNK_PAGES // 4):
            page0 = i * CHUNK_PAGES + j * 4
            at = page0 * PAGE
            s = dot_t(q_own[:, 0:latent], lat[page0 : page0 + 4].reshape(256, latent))
            s = s + dot_t(
                q_own[:, latent : latent + 128], keys[page0 : page0 + 4].reshape(256, 128)
            )
            b = bias[:, at : at + 256]
            s = (s.reshape(n_heads, reqs, 256) + b[None]).reshape(rows, 256)
            scores[:, at : at + 256] = s
            peak = jnp.maximum(s[:, 0:128], s[:, 128:256])
            top = peak if top is None else jnp.maximum(top, peak)
    top = jnp.max(top, axis=1, keepdims=True)

    for d in range(2):
        asks[d][2].wait_recv()
    c_sm = pltpu.make_async_copy(tab_in, tab_sm, sm_sem)
    c_sm.start()
    for d in range(2):
        asks[d][0].wait_recv()
        asks[d][1].wait_recv()
    for d in range(2):
        for h in range(n_heads):
            far = dot(qn_in[d, :, h * NOPE : (h + 1) * NOPE], wuk[h])
            at = pl.ds(d * n_heads + h, reqs, stride=2 * n_heads)
            for j in range(latent // 128):
                q_far[j, at, :] = far[:, j * 128 : (j + 1) * 128]
            q_far[latent // 128, at, :] = doubled_rope(qr_in.at[d], h)
    c_sm.wait()

    def pages_of(r):
        found = []
        for d in range(2):
            for j in range(LEND):
                found.append((tab_sm[d, r, j], tab_sm[d, r, LEND + j]))
        return found

    lane8 = iota((8, 128), 1)

    def far_scores(step, carry):
        for u in range(4):
            r = step * 4 + u
            found = pages_of(r)
            at = pl.ds(pl.multiple_of(r * 16, 16), 16)
            k_lat = jnp.concatenate(
                [lat[slot] for slot, _ in found], axis=0
            )
            k_rope = jnp.concatenate([keys[slot] for slot, _ in found], axis=0)
            q_lat = jnp.concatenate(
                [q_far[j, at, :] for j in range(latent // 128)], axis=1
            ).astype(BF16)
            s = dot_t(q_lat, k_lat) + dot_t(q_far[latent // 128, at, :].astype(BF16), k_rope)
            for d in range(2):
                limit = jnp.where(lane8 < 64, found[2 * d][1], found[2 * d + 1][1])
                part = s[d * 8 : (d + 1) * 8, d * 128 : (d + 1) * 128]
                part = jnp.where((lane8 & 63) < limit, part, NEG)
                s_far[pl.ds(pl.multiple_of(r * 16 + d * 8, 8), 8), :] = part
        return carry

    lax.fori_loop(0, reqs // 4, far_scores, 0)

    s = s_far[...]
    peak = jnp.maximum(jnp.max(s, axis=1, keepdims=True), -1e30)
    w = jnp.exp2((s - peak) * SCALE2)
    m_far[...] = jnp.broadcast_to(peak, s.shape)
    l_far[...] = jnp.broadcast_to(jnp.sum(w, axis=1, keepdims=True), s.shape)
    s_far[...] = w

    first_half = iota((16, 128), 0) < 8

    def far_values(step, carry):
        for u in range(4):
            r = step * 4 + u
            found = pages_of(r)
            at = pl.ds(pl.multiple_of(r * 16, 16), 16)
            w = s_far[at, :]
            w = jnp.concatenate(
                [jnp.where(first_half, w, 0.0), jnp.where(first_half, 0.0, w)], axis=1
            ).astype(BF16)
            v = jnp.concatenate(
                [lat[slot] for slot, _ in found], axis=0
            )
            o = dot(w, v)
            for j in range(latent // 128):
                o_far[j, at, :] = o[:, j * 128 : (j + 1) * 128]
        return carry

    lax.fori_loop(0, reqs // 4, far_values, 0)

    c_wuv.wait()
    packs = [jnp.zeros((reqs, 128), F32) for _ in range(2)]
    for h in range(n_heads):
        o = []
        for d in range(2):
            at = pl.ds(d * n_heads + h, reqs, stride=2 * n_heads)
            o.append(
                jnp.concatenate([o_far[j, at, :] for j in range(latent // 128)], axis=1)
            )
            packs[d] = jnp.where(lane == h, m_far[at, :], packs[d])
            packs[d] = jnp.where(lane == n_heads + h, l_far[at, :], packs[d])
        u = dot(jnp.concatenate(o, axis=0).astype(BF16), wuv[h]).astype(BF16)
        for d in range(2):
            u_out[d, :, h * VDIM : (h + 1) * VDIM] = u[d * reqs : (d + 1) * reqs]
    for d in range(2):
        ml_out[d] = packs[d]

    backs = []
    for d, target in ((0, nxt), (1, prv)):
        duo = []
        for i, (src, dst) in enumerate(((ml_out, ml_in), (u_out, u_in))):
            copy = pltpu.make_async_remote_copy(
                src_ref=src.at[d], dst_ref=dst.at[d],
                send_sem=usend_sem.at[d, i], recv_sem=urecv_sem.at[d, i],
                device_id={"dp": target}, device_id_type=MESH,
            )
            copy.start()
            duo.append(copy)
        backs.append(duo)

    total = jnp.zeros((rows, 128), F32)
    for i in range(slots // CHUNK_PAGES):
        for j in range(CHUNK_PAGES // 2):
            at = i * chunk + j * 128
            w = jnp.exp2((scores[:, at : at + 128] - top) * SCALE2)
            total = total + w
            probs[:, at : at + 128] = w.astype(BF16)
        part = dot(probs[:, i * chunk : (i + 1) * chunk], lat[i * CHUNK_PAGES : (i + 1) * CHUNK_PAGES].reshape(chunk, latent))
        if i == 0:
            acc[...] = part
        else:
            acc[...] += part
    total = jnp.sum(total, axis=1, keepdims=True)

    own_u = []
    for h in range(n_heads):
        own_u.append(dot(acc[h * reqs : (h + 1) * reqs, :].astype(BF16), wuv[h]))

    for d in range(2):
        for copy in backs[d]:
            copy.wait_recv()
    for h in range(n_heads):
        mine = slice(h * reqs, (h + 1) * reqs)
        ms = [top[mine]] + [ml_in[d, :, h : h + 1] for d in range(2)]
        ls = [total[mine]] + [ml_in[d, :, n_heads + h : n_heads + h + 1] for d in range(2)]
        us = [own_u[h]] + [
            u_in[d, :, h * VDIM : (h + 1) * VDIM].astype(F32) for d in range(2)
        ]
        peak = jnp.maximum(jnp.maximum(ms[0], ms[1]), ms[2])
        fs = [jnp.exp2((m - peak) * SCALE2) for m in ms]
        den = fs[0] * ls[0] + fs[1] * ls[1] + fs[2] * ls[2]
        num = fs[0] * us[0] + fs[1] * us[1] + fs[2] * us[2]
        heads_out[:, h * VDIM : (h + 1) * VDIM] = (num / den).astype(BF16)

    c_wo0.wait()
    c_wo1.wait()
    y_out[...] = dot(heads_out[...], wo[0]).astype(BF16)
    c_y = pltpu.make_async_remote_copy(
        src_ref=y_out, dst_ref=y_in, send_sem=ysend_sem, recv_sem=yrecv_sem,
        device_id={"tp": 1 - side}, device_id_type=MESH,
    )
    c_y.start()
    mine = dot(heads_out[...], wo[1])
    c_y.wait()
    out_ref[...] = (mine + y_in[...].astype(F32)).astype(BF16)
    for d in range(2):
        for copy in asks[d]:
            copy.wait_send()
        for copy in backs[d]:
            copy.wait_send()


def shards(
    n_dp, q_nope, q_rope, lengths, page_table, lend_counts, latent_pages, rope_pages, w_uk, w_uv, w_o
):
    reqs = lengths.shape[0]
    slots, _, latent = latent_pages.shape
    n_heads = w_uk.shape[0]
    half = w_o.shape[1] // 2
    rows = reqs * n_heads
    tokens = slots * PAGE
    tab = jnp.concatenate(
        [page_table, lend_counts, lengths[:, None], jnp.zeros((reqs, 117), jnp.int32)], axis=1
    )
    vmem = pltpu.VMEM
    dma = pltpu.SemaphoreType.DMA
    n_chunks = slots // CHUNK_PAGES
    return pl.pallas_call(
        functools.partial(kernel, n_dp),
        out_shape=jax.ShapeDtypeStruct((reqs, half), BF16),
        in_specs=[pl.BlockSpec(memory_space=pl.ANY)] * 8,
        out_specs=pl.BlockSpec(memory_space=vmem),
        scratch_shapes=[
            vmem(q_nope.shape, BF16),
            vmem(q_rope.shape, BF16),
            vmem((reqs, 128), jnp.int32),
            vmem((2, reqs, 128), jnp.int32),
            vmem((slots, PAGE, latent), BF16),
            vmem(rope_pages.shape, BF16),
            vmem(w_uk.shape, BF16),
            vmem(w_uv.shape, BF16),
            vmem((2, w_o.shape[0], half), BF16),
            vmem((2, *q_nope.shape), BF16),
            vmem((2, *q_rope.shape), BF16),
            vmem((2, reqs, 128), jnp.int32),
            pltpu.SMEM((2, reqs, 128), jnp.int32),
            vmem((512, 256), BF16),
            vmem((slots, PAGE, 128), BF16),
            vmem((rows, latent + 128), BF16),
            vmem((reqs, tokens), F32),
            vmem((rows, tokens), F32),
            vmem((rows, tokens), BF16),
            vmem((rows, latent), F32),
            vmem((latent // 128 + 1, 2 * rows, 128), F32),
            vmem((2 * rows, 128), F32),
            vmem((latent // 128, 2 * rows, 128), F32),
            vmem((2 * rows, 128), F32),
            vmem((2 * rows, 128), F32),
            vmem((2, reqs, n_heads * VDIM), BF16),
            vmem((2, reqs, 128), F32),
            vmem((2, reqs, n_heads * VDIM), BF16),
            vmem((2, reqs, 128), F32),
            vmem((reqs, n_heads * VDIM), BF16),
            vmem((reqs, half), BF16),
            vmem((reqs, half), BF16),
            dma((8,)),
            dma((n_chunks,)),
            dma,
            dma((2, 3)),
            dma((2, 3)),
            dma((2, 2)),
            dma((2, 2)),
            dma,
            dma,
        ],
        compiler_params=pltpu.CompilerParams(
            collective_id=0, has_side_effects=True, vmem_limit_bytes=60 * 1024 * 1024
        ),
        name="latent_step",
    )(
        q_nope, q_rope, tab, latent_pages, rope_pages, w_uk, w_uv, w_o
    )


def solution(mesh):
    in_specs = (
        P("dp", "tp"),
        P("dp", "tp"),
        P("dp"),
        P("dp", None),
        P("dp", None),
        P("dp", None, None),
        P("dp", None),
        P("tp", None, None),
        P("tp", None, None),
        P("tp", None),
    )
    return jax.shard_map(
        functools.partial(shards, mesh.shape["dp"]),
        mesh=mesh, in_specs=in_specs, out_specs=P("dp", "tp"), check_vma=False,
    )
```

time: 114 us -> 37.3 us (0.33)
  the two profiles are of different devices: /device:TPU:1 before, /device:TPU:0 now
where the time goes in v1:
time: 37.3 us; the launch traced here: 37.1 us
  Pallas kernels  32.6 us (87%)
  local copies, waits for them, and re-layouts  3.81 us (10%)
  other arithmetic  0.69 us (2%)
    pallas_call x1, Pallas kernels, shards(): pl.pallas_call(functools.partial(kernel, n_dp), out_shape=jax.ShapeDtypeS...  32.6 us
    unnamed x3, local copies, waits for them, and re-layouts  2.99 us

profile of v1, /device:TPU:0, one launch (start us, length us, event | category | flops | bytes accessed | tf_op | source)
XLA Modules:
  0.0 37.1 jit_solution(13961179550925247)
XLA Ops:
  0.0 0.1 pad.3.clone
  0.1 0.7 %copy.13 = s32[32,1]{1,0:T(8,128)S(1)} copy(s32[32,1]{0,1:T(1,128)} %bitcast.1) | data formatting | bytes 256 | tf_op jit(solution)/shard_map/broadcast_in_dim | solution.py:358
  0.8 0.8 %copy.11 = s32[32,8]{1,0:T(8,128)S(1)} copy(s32[32,8]{0,1:T(8,128)} %param.13) | data formatting | bytes 2048 | tf_op args[3]
  1.6 0.8 %copy.12 = s32[32,2]{1,0:T(8,128)S(1)} copy(s32[32,2]{0,1:T(2,128)} %param.14) | data formatting | bytes 512 | tf_op args[4]
  2.3 0.7 %add_add_fusion.tab_hbm = s32[32,128]{1,0:T(8,128)} fusion(s32[32,1]{1,0:T(8,128)S(1)} %copy.13, s32[32,2]{1,0:T(8,128)S(1)} %copy.12, s32[32,8]{1,0:T(8,128)S(1)} %copy.11, s32[128]{0:T(128)S(1)} %pad.3.clone), kind=kLoop, calls=%fused_computation | loop fusion | flops 12288 | bytes 18304 | tf_op jit(solution)/shard_map/concatenate | solution.py:357
  3.0 32.6 %latent_step.1 = bf16[32,1024]{1,0:T(8,128)(2,1)} custom-call(bf16[32,1024]{1,0:T(8,128)(2,1)} %qn_hbm.1, bf16[32,512]{1,0:T(8,128)(2,1)} %qr_hbm.1, s32[32,128]{1,0:T(8,128)} %add_add_fusion.tab_hbm, bf16[96,64,512]{2,1,0:T(8,128)(2,1)} %lat_hbm.1, bf16[96,4096]{1,0:T(8,128)(2,1)} %rope_hbm.1, bf16[8,128,512]{2,1,0:T(8,128)(2,1)} %wuk_hbm.1, ...), custom_call_target="tpu_custom_call" | custom-call | tf_op jit(solution)/shard_map/latent_step/pallas_call | solution.py:363
  35.6 1.5 %copy.15 = bf16[32,1024]{1,0:T(8,128)(2,1)} copy(bf16[32,1024]{1,0:T(8,128)(2,1)} %latent_step.1) | data formatting | bytes 131072
  (1 shorter events, 0.0 us)

commit v2 on v1

v2 whole, which is shorter than its diff:
```python
import functools
import math

import jax
import jax.numpy as jnp
from jax import lax
from jax.experimental import pallas as pl
from jax.experimental.pallas import tpu as pltpu
from jax.sharding import PartitionSpec as P

ROPE = 64
NOPE = 128
VDIM = 128
PAGE = 64
MAXP = 8
LEND = 2
MESH = pl.DeviceIdType.MESH
NEG = -3e38
SCALE2 = math.log2(math.e) / math.sqrt(NOPE + ROPE)
GROUP = 4
PARTS = 2
F32 = jnp.float32
BF16 = jnp.bfloat16

def dot(a, b):
    return lax.dot_general(a, b, (((1,), (0,)), ((), ())), preferred_element_type=F32)

def dot_t(a, b):
    return lax.dot_general(a, b, (((1,), (1,)), ((), ())), preferred_element_type=F32)

def iota(shape, dim):
    return lax.broadcasted_iota(jnp.int32, shape, dim)

def doubled_rope(q_rope, head):
    pair = q_rope[:, (head // 2) * 128 : (head // 2 + 1) * 128].astype(F32)
    turned = pltpu.roll(pair, 64, 1)
    low = iota(pair.shape, 1) < 64
    return jnp.where(low, pair, turned) if head % 2 == 0 else jnp.where(low, turned, pair)

def kernel(
    n_dp,
    qn_hbm, qr_hbm, table_hbm, lent_hbm, size_hbm, lat_hbm, rope_hbm, wuk_hbm, wuv_hbm, wo_hbm,
    out_ref,
    qn, qr, table, lent, size, plan, lat, rope, wuk, wuv, wo,
    qn_in, qr_in, plan_in, plan_sm,
    perm, keys, q_own, bias, scores, peaks, probs, acc,
    q_far, o_far, m_far, l_far,
    u_out, ml_out, u_in, ml_in, heads_out, y_out, y_in,
    load_sem, sm_sem, qsend_sem, qrecv_sem, usend_sem, urecv_sem, ysend_sem, yrecv_sem,
):
    reqs = qn.shape[0]
    n_heads = wuk.shape[0]
    slots = rope.shape[0]
    latent = lat.shape[2]
    wide = latent // 128
    half = out_ref.shape[1]
    rows = reqs * n_heads
    parts = y_out.shape[0]
    piece = half // parts

    me = lax.axis_index("dp")
    side = lax.axis_index("tp")
    nxt = lax.rem(me + 1, n_dp)
    prv = lax.rem(me + n_dp - 1, n_dp)
    near = jnp.where(me == 1, 0, lax.rem(me, 2))

    def local(src, dst, i):
        copy = pltpu.make_async_copy(src, dst, load_sem.at[i])
        copy.start()
        return copy

    barrier = pltpu.get_barrier_semaphore()
    pl.semaphore_signal(barrier, inc=1, device_id={"dp": prv}, device_id_type=MESH)
    pl.semaphore_signal(barrier, inc=1, device_id={"dp": nxt}, device_id_type=MESH)
    pl.semaphore_signal(barrier, inc=1, device_id={"tp": 1 - side}, device_id_type=MESH)
    c_table = local(table_hbm, table, 0)
    c_lent = local(lent_hbm, lent, 1)
    c_size = local(size_hbm, size, 2)
    c_rope = local(rope_hbm, rope, 5)
    c_qn = local(qn_hbm, qn, 3)
    c_qr = local(qr_hbm, qr, 4)
    c_wuk = local(wuk_hbm, wuk, 6)
    thirds = slots // 3
    c_lat = [
        local(lat_hbm.at[pl.ds(i * thirds, thirds)], lat.at[pl.ds(i * thirds, thirds)], 7 + i)
        for i in range(3)
    ]

    out_row = iota((512, 256), 0)
    in_row = iota((512, 256), 1)
    hit = ((out_row >> 5) == (in_row & 15)) & (((out_row & 31) >> 1) == (in_row >> 4))
    perm[...] = jnp.where(hit, 1.0, 0.0).astype(BF16)

    c_table.wait()
    c_lent.wait()
    c_size.wait()

    def spread(row):
        return jnp.broadcast_to(row, (8, reqs))

    row8 = iota((8, reqs), 0)
    pages = table[...]
    length = spread(size[...])
    lent_left = spread(lent[0:1, :])
    lent_right = spread(lent[1:2, :])
    n_pages = (length + (PAGE - 1)) >> 6
    first = n_pages - lent_left - lent_right
    for d in range(2):
        start = first if d == 0 else n_pages - lent_right
        held = lent_left if d == 0 else lent_right
        packed = jnp.zeros((8, reqs), jnp.int32)
        for j in range(LEND):
            at = start + j
            slot = spread(jnp.sum(jnp.where(row8 == at, pages, 0), axis=0, keepdims=True))
            used = held > j
            slot = jnp.where(used, jnp.clip(slot, 0, slots - 1), 0)
            live = jnp.where(used, jnp.clip(length - at * PAGE, 0, PAGE), 0)
            packed = jnp.where(row8 == j, slot, packed)
            packed = jnp.where(row8 == LEND + j, live, packed)
        plan[d, :, 0:reqs] = packed

    lane = iota((reqs, 128), 1)
    facts = jnp.concatenate([pages, first, length], axis=0).astype(F32)
    facts = jnp.concatenate([facts, jnp.zeros((24, 128 - reqs), F32)], axis=1)
    facts = jnp.concatenate([facts, jnp.zeros((104, 128), F32)], axis=0)
    facts = jnp.transpose(facts)[0:reqs].astype(jnp.int32)

    def column(i):
        return jnp.broadcast_to(facts[:, i : i + 1], (reqs, 128))

    first = column(8)
    length = column(16)
    count = jnp.zeros((reqs, 128), jnp.int32)
    for k in range(MAXP):
        live = jnp.clip(length - k * PAGE, 0, PAGE)
        count = count + jnp.where((lane == column(k)) & (first > k), live, 0)
    for g in range(slots // 2):
        even = jnp.broadcast_to(count[:, 2 * g : 2 * g + 1], (reqs, 128))
        odd = jnp.broadcast_to(count[:, 2 * g + 1 : 2 * g + 2], (reqs, 128))
        limit = jnp.where(lane < 64, even, odd)
        bias[:, g * 128 : (g + 1) * 128] = jnp.where((lane & 63) < limit, 0.0, NEG)

    c_rope.wait()
    row_odd = (iota((512, 128), 0) & 1) == 1
    lane_high = iota((512, 128), 1) >= 64
    keep = row_odd == lane_high
    for g in range(slots // 16):
        page_rows = pl.ds(g * 16, 16)
        left = jnp.concatenate(
            [rope[page_rows, j * 128 : (j + 1) * 128] for j in range(16)], axis=0
        )
        right = jnp.concatenate(
            [rope[page_rows, (16 + j) * 128 : (17 + j) * 128] for j in range(16)], axis=0
        )
        moved = dot(perm[...], jnp.concatenate([left, right], axis=1))
        for s in range(2):
            part = jnp.where(keep, moved[:, s * 128 : (s + 1) * 128], 0.0).astype(BF16)
            keys[page_rows, s * 32 : (s + 1) * 32, :] = part.reshape(16, 32, 128)

    c_qn.wait()
    c_qr.wait()

    def pool_ready():
        c_wuk.wait()
        for copy in c_lat:
            copy.wait()

    def own_scores():
        for h in range(n_heads):
            mine = pl.ds(h * reqs, reqs)
            q_own[mine, 0:latent] = dot(qn[:, h * NOPE : (h + 1) * NOPE], wuk[h]).astype(BF16)
            q_own[mine, latent : latent + 128] = doubled_rope(qr, h).astype(BF16)
        top = None
        for i in range(slots // 4):
            at = i * 4 * PAGE
            s = dot_t(q_own[:, 0:latent], lat[i * 4 : i * 4 + 4].reshape(256, latent))
            s = s + dot_t(
                q_own[:, latent : latent + 128], keys[i * 4 : i * 4 + 4].reshape(256, 128)
            )
            b = bias[:, at : at + 256]
            s = (s.reshape(n_heads, reqs, 256) + b[None]).reshape(rows, 256)
            scores[:, at : at + 256] = s
            peak = jnp.maximum(s[:, 0:128], s[:, 128:256])
            top = peak if top is None else jnp.maximum(top, peak)
        peaks[...] = top

    def early_scores():
        pool_ready()
        own_scores()

    pl.when(me <= 1)(early_scores)

    pl.semaphore_wait(barrier, 3)

    def ask(d, i, src, dst):
        return pltpu.make_async_remote_copy(
            src_ref=src, dst_ref=dst.at[d],
            send_sem=qsend_sem.at[d, i], recv_sem=qrecv_sem.at[d, i],
            device_id={"dp": prv if isinstance(d, int) and d == 0 else nxt}, device_id_type=MESH,
        )

    asks = []
    for d in range(2):
        asks.append(ask(d, 2, plan.at[d], plan_in))
        asks.append(ask(d, 0, qn, qn_in))
        asks.append(ask(d, 1, qr, qr_in))
    for copy in asks:
        copy.start()
    c_wuv = local(wuv_hbm, wuv, 10)
    c_wo = [
        local(
            wo_hbm.at[:, pl.ds((1 - side) * half + p * piece, piece)], wo.at[p], 11 + p
        )
        for p in range(parts)
    ] + [
        local(wo_hbm.at[:, pl.ds(side * half + p * piece, piece)], wo.at[parts + p], 11 + parts + p)
        for p in range(parts)
    ]

    pl.when(me > 1)(pool_ready)
    lane8 = iota((8, 128), 1)

    def far_terms(d, wuv_copy):
        ask(d, 2, plan.at[0], plan_in).wait_recv()
        c_sm = pltpu.make_async_copy(plan_in.at[d], plan_sm.at[d], sm_sem.at[d])
        c_sm.start()
        ask(d, 0, qn, qn_in).wait_recv()
        ask(d, 1, qr, qr_in).wait_recv()
        q_rope = qr_in[d]
        for h in range(n_heads):
            far = dot(qn_in[d, :, h * NOPE : (h + 1) * NOPE], wuk[h])
            at = pl.ds(h, reqs, stride=n_heads)
            for j in range(wide):
                q_far[j, at, :] = far[:, j * 128 : (j + 1) * 128]
            q_far[wide, at, :] = doubled_rope(q_rope, h)
        c_sm.wait()

        def held(pair):
            return [
                (plan_sm[d, j, r], plan_sm[d, LEND + j, r])
                for r in (2 * pair, 2 * pair + 1)
                for j in range(LEND)
            ]

        def far_weights(pair):
            found = held(pair)
            at = slice(pair * 16, pair * 16 + 16)
            k_lat = jnp.concatenate([lat[slot] for slot, _ in found], axis=0)
            k_rope = jnp.concatenate([keys[slot] for slot, _ in found], axis=0)
            q_lat = jnp.concatenate([q_far[j, at, :] for j in range(wide)], axis=1).astype(BF16)
            s = dot_t(q_lat, k_lat) + dot_t(q_far[wide, at, :].astype(BF16), k_rope)
            blocks = []
            for e in range(2):
                limit = jnp.where(lane8 < 64, found[2 * e][1], found[2 * e + 1][1])
                part = s[e * 8 : (e + 1) * 8, e * 128 : (e + 1) * 128]
                part = jnp.where((lane8 & 63) < limit, part, NEG)
                peak = jnp.maximum(jnp.max(part, axis=1, keepdims=True), -1e30)
                w = jnp.exp2((part - peak) * SCALE2)
                total = jnp.sum(w, axis=1, keepdims=True)
                here = slice(pair * 16 + e * 8, pair * 16 + e * 8 + 8)
                m_far[here, :] = jnp.broadcast_to(peak, (8, 128))
                l_far[here, :] = jnp.broadcast_to(total, (8, 128))
                blocks.append(w)
            return blocks

        def far_values(pair, blocks):
            found = held(pair)
            none = jnp.zeros((8, 128), F32)
            w = jnp.concatenate(
                [
                    jnp.concatenate([blocks[0], none], axis=1),
                    jnp.concatenate([none, blocks[1]], axis=1),
                ],
                axis=0,
            ).astype(BF16)
            o = dot(w, jnp.concatenate([lat[slot] for slot, _ in found], axis=0))
            for j in range(wide):
                o_far[j, pair * 16 : pair * 16 + 16, :] = o[:, j * 128 : (j + 1) * 128]

        pairs = reqs // 2
        waiting = {}
        for pair in range(pairs + GROUP):
            if pair < pairs:
                waiting[pair] = far_weights(pair)
            if pair >= GROUP:
                far_values(pair - GROUP, waiting.pop(pair - GROUP))

        if wuv_copy is not None:
            wuv_copy.wait()
        pack = jnp.zeros((reqs, 128), F32)
        for h in range(n_heads):
            at = pl.ds(h, reqs, stride=n_heads)
            o = jnp.concatenate([o_far[j, at, :] for j in range(wide)], axis=1)
            u_out[d, :, h * VDIM : (h + 1) * VDIM] = dot(o.astype(BF16), wuv[h]).astype(BF16)
            pack = jnp.where(lane == h, m_far[at, :], pack)
            pack = jnp.where(lane == n_heads + h, l_far[at, :], pack)
        ml_out[d] = pack
        backs = []
        for i, (src, dst) in enumerate(((ml_out, ml_in), (u_out, u_in))):
            copy = pltpu.make_async_remote_copy(
                src_ref=src.at[d], dst_ref=dst.at[d],
                send_sem=usend_sem.at[d, i], recv_sem=urecv_sem.at[d, i],
                device_id={"dp": jnp.where(d == 0, nxt, prv)}, device_id_type=MESH,
            )
            copy.start()
            backs.append(copy)
        return backs

    backs = far_terms(near, c_wuv)

    backs += far_terms(1 - near, None)

    pl.when(me > 1)(own_scores)


    top = jnp.max(peaks[...], axis=1, keepdims=True)
    total = jnp.zeros((rows, 128), F32)
    span = 16 * PAGE
    for i in range(slots // 16):
        for j in range(span // 128):
            at = i * span + j * 128
            w = jnp.exp2((scores[:, at : at + 128] - top) * SCALE2)
            total = total + w
            probs[:, at : at + 128] = w.astype(BF16)
        part = dot(
            probs[:, i * span : (i + 1) * span], lat[i * 16 : (i + 1) * 16].reshape(span, latent)
        )
        if i == 0:
            acc[...] = part
        else:
            acc[...] += part
    total = jnp.sum(total, axis=1, keepdims=True)

    own_u = []
    m_own = jnp.zeros((reqs, 128), F32)
    l_own = jnp.zeros((reqs, 128), F32)
    for h in range(n_heads):
        mine = slice(h * reqs, (h + 1) * reqs)
        own_u.append(dot(acc[mine, :].astype(BF16), wuv[h]))
        m_own = jnp.where(lane == h, top[mine], m_own)
        l_own = jnp.where(lane == h, total[mine], l_own)

    for d in range(2):
        for i, (src, dst) in enumerate(((ml_out, ml_in), (u_out, u_in))):
            pltpu.make_async_remote_copy(
                src_ref=src.at[d], dst_ref=dst.at[d],
                send_sem=usend_sem.at[d, i], recv_sem=urecv_sem.at[d, i],
                device_id={"dp": nxt}, device_id_type=MESH,
            ).wait_recv()

    for copy in c_wo:
        copy.wait()

    ms = [m_own, ml_in[0], ml_in[1]]
    ls = [l_own] + [pltpu.roll(ml_in[d], 128 - n_heads, 1) for d in range(2)]
    peak = jnp.maximum(jnp.maximum(ms[0], ms[1]), ms[2])
    fs = [jnp.where(lane < n_heads, jnp.exp2((m - peak) * SCALE2), 1.0) for m in ms]
    ls = [jnp.where(lane < n_heads, one, 1.0) for one in ls]
    share = 1.0 / (fs[0] * ls[0] + fs[1] * ls[1] + fs[2] * ls[2])
    fs = [f * share for f in fs]
    for h in range(n_heads):
        at = slice(h * VDIM, (h + 1) * VDIM)
        us = [own_u[h], u_in[0, :, at].astype(F32), u_in[1, :, at].astype(F32)]
        gs = [jnp.broadcast_to(f[:, h : h + 1], (reqs, VDIM)) for f in fs]
        heads_out[:, at] = (gs[0] * us[0] + gs[1] * us[1] + gs[2] * us[2]).astype(BF16)

    sends = []
    for p in range(parts):
        y_out[p] = dot(heads_out[...], wo[p]).astype(BF16)
        copy = pltpu.make_async_remote_copy(
            src_ref=y_out.at[p], dst_ref=y_in.at[p],
            send_sem=ysend_sem.at[p], recv_sem=yrecv_sem.at[p],
            device_id={"tp": 1 - side}, device_id_type=MESH,
        )
        copy.start()
        sends.append(copy)
    mine = [dot(heads_out[...], wo[parts + p]) for p in range(parts)]

    for p in range(parts):
        sends[p].wait_recv()
        out_ref[:, p * piece : (p + 1) * piece] = (mine[p] + y_in[p].astype(F32)).astype(BF16)
    for copy in asks + backs + sends:
        copy.wait_send()

def shards(
    n_dp, q_nope, q_rope, lengths, page_table, lend_counts, latent_pages, rope_pages, w_uk, w_uv, w_o
):
    reqs = lengths.shape[0]
    slots, _, latent = latent_pages.shape
    n_heads = w_uk.shape[0]
    half = w_o.shape[1] // 2
    rows = reqs * n_heads
    tokens = slots * PAGE
    vmem = pltpu.VMEM
    dma = pltpu.SemaphoreType.DMA
    return pl.pallas_call(
        functools.partial(kernel, n_dp),
        out_shape=jax.ShapeDtypeStruct((reqs, half), BF16),
        in_specs=[pl.BlockSpec(memory_space=pltpu.HBM)] * 10,
        out_specs=pl.BlockSpec(memory_space=vmem),
        scratch_shapes=[
            vmem(q_nope.shape, BF16),
            vmem(q_rope.shape, BF16),
            vmem((MAXP, reqs), jnp.int32),
            vmem((2, reqs), jnp.int32),
            vmem((1, reqs), jnp.int32),
            vmem((2, 8, 128), jnp.int32),
            vmem((slots, PAGE, latent), BF16),
            vmem(rope_pages.shape, BF16),
            vmem(w_uk.shape, BF16),
            vmem(w_uv.shape, BF16),
            vmem((2 * PARTS, w_o.shape[0], half // PARTS), BF16),
            vmem((2, *q_nope.shape), BF16),
            vmem((2, *q_rope.shape), BF16),
            vmem((2, 8, 128), jnp.int32),
            pltpu.SMEM((2, 8, 128), jnp.int32),
            vmem((512, 256), BF16),
            vmem((slots, PAGE, 128), BF16),
            vmem((rows, latent + 128), BF16),
            vmem((reqs, tokens), F32),
            vmem((rows, tokens), F32),
            vmem((rows, 128), F32),
            vmem((rows, tokens), BF16),
            vmem((rows, latent), F32),
            vmem((latent // 128 + 1, rows, 128), F32),
            vmem((latent // 128, rows, 128), F32),
            vmem((rows, 128), F32),
            vmem((rows, 128), F32),
            vmem((2, reqs, n_heads * VDIM), BF16),
            vmem((2, reqs, 128), F32),
            vmem((2, reqs, n_heads * VDIM), BF16),
            vmem((2, reqs, 128), F32),
            vmem((reqs, n_heads * VDIM), BF16),
            vmem((PARTS, reqs, half // PARTS), BF16),
            vmem((PARTS, reqs, half // PARTS), BF16),
            dma((11 + 2 * PARTS,)),
            dma((2,)),
            dma((2, 3)),
            dma((2, 3)),
            dma((2, 2)),
            dma((2, 2)),
            dma((PARTS,)),
            dma((PARTS,)),
        ],
        compiler_params=pltpu.CompilerParams(
            collective_id=0, has_side_effects=True, vmem_limit_bytes=44 * 1024 * 1024
        ),
        name="latent_step",
    )(
        *(
            pltpu.with_memory_space_constraint(x, pltpu.HBM)
            for x in (
                q_nope, q_rope, page_table.T, lend_counts.T, lengths.reshape(1, reqs),
                latent_pages, rope_pages, w_uk, w_uv, w_o,
            )
        )
    )

def solution(mesh):
    in_specs = (
        P("dp", "tp"),
        P("dp", "tp"),
        P("dp"),
        P("dp", None),
        P("dp", None),
        P("dp", None, None),
        P("dp", None),
        P("tp", None, None),
        P("tp", None, None),
        P("tp", None),
    )
    return jax.shard_map(
        functools.partial(shards, mesh.shape["dp"]),
        mesh=mesh, in_specs=in_specs, out_specs=P("dp", "tp"), check_vma=False,
    )
```

time: 37.3 us -> 27 us (0.72)
  Pallas kernels: 32.6 us -> 26.2 us
  local copies, waits for them, and re-layouts: 3.81 us -> 0.63 us
  other arithmetic: 0.69 us -> 0 us
    pallas_call x1, Pallas kernels: 32.6 us -> 26.2 us  [shards(): pl.pallas_call(functools.partial(kernel, n_dp), out_shape=jax.ShapeDtypeS...]
    unnamed x3 -> x1, local copies, waits for them, and re-layouts: 2.99 us -> 0.63 us
    broadcast_in_dim x2 -> x0, local copies, waits for them, and re-layouts: 0.74 us -> none  [the longest x1 0.74 us: shards(): lengths[:, None]]
    concatenate x1 -> x0, other arithmetic: 0.69 us -> none  [shards(): jnp.concatenate([page_table, lend_counts, lengths[:, None], jnp.zeros((re...]
where the time goes in v2:
time: 27 us; the launch traced here: 26.9 us
  Pallas kernels  26.2 us (97%)
  local copies, waits for them, and re-layouts  0.63 us (2%)
    pallas_call x1, Pallas kernels, shards(): pl.pallas_call(functools.partial(kernel, n_dp), out_shape=jax.ShapeDtypeS...  26.2 us
    unnamed x1, local copies, waits for them, and re-layouts  0.63 us

profile of v2, /device:TPU:0, one launch (start us, length us, event | category | flops | bytes accessed | tf_op | source)
XLA Modules:
  0.0 26.9 jit_solution(2197354499892679008)
XLA Ops:
  0.0 26.2 %latent_step.1 = bf16[32,1024]{1,0:T(8,128)(2,1)S(1)} custom-call(bf16[32,1024]{1,0:T(8,128)(2,1)} %qn_hbm.1, bf16[32,512]{1,0:T(8,128)(2,1)} %qr_hbm.1, s32[8,32]{1,0:T(8,128)} %bitcast.3, s32[2,32]{1,0:T(2,128)} %bitcast.4, s32[1,32]{1,0:T(1,128)} %bitcast.5, bf16[96,64,512]{2,1,0:T(8,128)(2,1)} %lat_hbm.1, bf16[96,4096]{1,0:T(8,128)(2,1)} %rope_hbm.1, ...), custom_call_target="tpu_custom_call" | custom-call | tf_op jit(solution)/shard_map/latent_step/pallas_call | solution.py:396
  26.2 0.6 %copy.12 = bf16[32,1024]{1,0:T(8,128)(2,1)} copy(bf16[32,1024]{1,0:T(8,128)(2,1)S(1)} %latent_step.1) | data formatting | bytes 131072

commit v3 on v2

--- a/solution.py
+++ b/solution.py
@@ -17,8 +17,10 @@
 MESH = pl.DeviceIdType.MESH
 NEG = -3e38
 SCALE2 = math.log2(math.e) / math.sqrt(NOPE + ROPE)
-GROUP = 4
+GROUP = 8
 PARTS = 2
+POOL_COPIES = 8
+RELAY = 15
 F32 = jnp.float32
 BF16 = jnp.bfloat16
 
@@ -38,15 +40,15 @@
     return jnp.where(low, pair, turned) if head % 2 == 0 else jnp.where(low, turned, pair)
 
 def kernel(
-    n_dp,
+    n_dp, relay,
     qn_hbm, qr_hbm, table_hbm, lent_hbm, size_hbm, lat_hbm, rope_hbm, wuk_hbm, wuv_hbm, wo_hbm,
     out_ref,
     qn, qr, table, lent, size, plan, lat, rope, wuk, wuv, wo,
-    qn_in, qr_in, plan_in, plan_sm,
-    perm, keys, q_own, bias, scores, peaks, probs, acc,
+    qn_in, qr_in, plan_in, qn_by, qr_by, plan_by, plan_sm,
+    perm, keys, q_own, bias, scores, peaks, totals, probs, acc,
     q_far, o_far, m_far, l_far,
     u_out, ml_out, u_in, ml_in, heads_out, y_out, y_in,
-    load_sem, sm_sem, qsend_sem, qrecv_sem, usend_sem, urecv_sem, ysend_sem, yrecv_sem,
+    load_sem, sm_sem, gate_sem, bysend_sem, byrecv_sem, qsend_sem, qrecv_sem, usend_sem, urecv_sem, ysend_sem, yrecv_sem,
 ):
     reqs = qn.shape[0]
     n_heads = wuk.shape[0]
@@ -62,7 +64,8 @@
     side = lax.axis_index("tp")
     nxt = lax.rem(me + 1, n_dp)
     prv = lax.rem(me + n_dp - 1, n_dp)
-    near = jnp.where(me == 1, 0, lax.rem(me, 2))
+    last = n_dp - 1
+    near = jnp.where((me == 1) | (me == last), 0, lax.rem(me, 2))
 
     def local(src, dst, i):
         copy = pltpu.make_async_copy(src, dst, load_sem.at[i])
@@ -70,9 +73,19 @@
         return copy
 
     barrier = pltpu.get_barrier_semaphore()
-    pl.semaphore_signal(barrier, inc=1, device_id={"dp": prv}, device_id_type=MESH)
-    pl.semaphore_signal(barrier, inc=1, device_id={"dp": nxt}, device_id_type=MESH)
-    pl.semaphore_signal(barrier, inc=1, device_id={"tp": 1 - side}, device_id_type=MESH)
+
+    def arrive(**target):
+        pl.semaphore_signal(barrier, inc=1, device_id=target, device_id_type=MESH)
+
+    pl.when(me != last)(lambda: arrive(dp=nxt))
+    arrive(dp=prv)
+    arrive(tp=1 - side)
+
+    @pl.when(me == relay)
+    def _():
+        arrive(dp=last)
+        arrive(dp=0)
+
     c_table = local(table_hbm, table, 0)
     c_lent = local(lent_hbm, lent, 1)
     c_size = local(size_hbm, size, 2)
@@ -80,10 +93,11 @@
     c_qn = local(qn_hbm, qn, 3)
     c_qr = local(qr_hbm, qr, 4)
     c_wuk = local(wuk_hbm, wuk, 6)
-    thirds = slots // 3
+    pool_at = 8 + 2 * parts
+    share = slots // POOL_COPIES
     c_lat = [
-        local(lat_hbm.at[pl.ds(i * thirds, thirds)], lat.at[pl.ds(i * thirds, thirds)], 7 + i)
-        for i in range(3)
+        local(lat_hbm.at[pl.ds(i * share, share)], lat.at[pl.ds(i * share, share)], pool_at + i)
+        for i in range(POOL_COPIES)
     ]
 
     out_row = iota((512, 256), 0)
@@ -119,27 +133,6 @@
             packed = jnp.where(row8 == LEND + j, live, packed)
         plan[d, :, 0:reqs] = packed
 
-    lane = iota((reqs, 128), 1)
-    facts = jnp.concatenate([pages, first, length], axis=0).astype(F32)
-    facts = jnp.concatenate([facts, jnp.zeros((24, 128 - reqs), F32)], axis=1)
-    facts = jnp.concatenate([facts, jnp.zeros((104, 128), F32)], axis=0)
-    facts = jnp.transpose(facts)[0:reqs].astype(jnp.int32)
-
-    def column(i):
-        return jnp.broadcast_to(facts[:, i : i + 1], (reqs, 128))
-
-    first = column(8)
-    length = column(16)
-    count = jnp.zeros((reqs, 128), jnp.int32)
-    for k in range(MAXP):
-        live = jnp.clip(length - k * PAGE, 0, PAGE)
-        count = count + jnp.where((lane == column(k)) & (first > k), live, 0)
-    for g in range(slots // 2):
-        even = jnp.broadcast_to(count[:, 2 * g : 2 * g + 1], (reqs, 128))
-        odd = jnp.broadcast_to(count[:, 2 * g + 1 : 2 * g + 2], (reqs, 128))
-        limit = jnp.where(lane < 64, even, odd)
-        bias[:, g * 128 : (g + 1) * 128] = jnp.where((lane & 63) < limit, 0.0, NEG)
-
     c_rope.wait()
     row_odd = (iota((512, 128), 0) & 1) == 1
     lane_high = iota((512, 128), 1) >= 64
@@ -184,13 +177,12 @@
             top = peak if top is None else jnp.maximum(top, peak)
         peaks[...] = top
 
-    def early_scores():
-        pool_ready()
-        own_scores()
-
-    pl.when(me <= 1)(early_scores)
-
-    pl.semaphore_wait(barrier, 3)
+    @pl.when(me == last)
+    def _():
+        pl.semaphore_wait(barrier, 4)
+        pl.semaphore_signal(gate_sem, inc=1, device_id={"dp": relay}, device_id_type=MESH)
+
+    pl.when(me != last)(lambda: pl.semaphore_wait(barrier, 3))
 
     def ask(d, i, src, dst):
         return pltpu.make_async_remote_copy(
@@ -204,35 +196,95 @@
         asks.append(ask(d, 2, plan.at[d], plan_in))
         asks.append(ask(d, 0, qn, qn_in))
         asks.append(ask(d, 1, qr, qr_in))
-    for copy in asks:
+
+    def to_relay(i):
+        src, dst = [(qn, qn_by), (qr, qr_by), (plan.at[0], plan_by)][i]
+        return pltpu.make_async_remote_copy(
+            src_ref=src, dst_ref=dst, send_sem=qsend_sem.at[0, i], recv_sem=byrecv_sem.at[i],
+            device_id={"dp": relay}, device_id_type=MESH,
+        )
+
+    def from_relay(i):
+        src, dst = [(qn_by, qn_in), (qr_by, qr_in), (plan_by, plan_in)][i]
+        return pltpu.make_async_remote_copy(
+            src_ref=src, dst_ref=dst.at[0], send_sem=bysend_sem.at[i], recv_sem=qrecv_sem.at[0, i],
+            device_id={"dp": last}, device_id_type=MESH,
+        )
+
+    @pl.when(me == 0)
+    def _():
+        for i in (2, 0, 1):
+            to_relay(i).start()
+
+    @pl.when(me != 0)
+    def _():
+        for copy in asks[:3]:
+            copy.start()
+
+    for copy in asks[3:]:
         copy.start()
-    c_wuv = local(wuv_hbm, wuv, 10)
+    c_wuv = local(wuv_hbm, wuv, 7)
     c_wo = [
         local(
-            wo_hbm.at[:, pl.ds((1 - side) * half + p * piece, piece)], wo.at[p], 11 + p
+            wo_hbm.at[:, pl.ds((1 - side) * half + p * piece, piece)], wo.at[p], 8 + p
         )
         for p in range(parts)
     ] + [
-        local(wo_hbm.at[:, pl.ds(side * half + p * piece, piece)], wo.at[parts + p], 11 + parts + p)
+        local(wo_hbm.at[:, pl.ds(side * half + p * piece, piece)], wo.at[parts + p], 8 + parts + p)
         for p in range(parts)
     ]
 
-    pl.when(me > 1)(pool_ready)
+    lane = iota((reqs, 128), 1)
+    facts = jnp.concatenate([pages, first, length], axis=0).astype(F32)
+    facts = jnp.concatenate([facts, jnp.zeros((24, 128 - reqs), F32)], axis=1)
+    facts = jnp.concatenate([facts, jnp.zeros((104, 128), F32)], axis=0)
+    facts = jnp.transpose(facts)[0:reqs].astype(jnp.int32)
+
+    def column(i):
+        return jnp.broadcast_to(facts[:, i : i + 1], (reqs, 128))
+
+    first = column(8)
+    length = column(16)
+    count = jnp.zeros((reqs, 128), jnp.int32)
+    for k in range(MAXP):
+        live = jnp.clip(length - k * PAGE, 0, PAGE)
+        count = count + jnp.where((lane == column(k)) & (first > k), live, 0)
+    for g in range(slots // 2):
+        even = jnp.broadcast_to(count[:, 2 * g : 2 * g + 1], (reqs, 128))
+        odd = jnp.broadcast_to(count[:, 2 * g + 1 : 2 * g + 2], (reqs, 128))
+        limit = jnp.where(lane < 64, even, odd)
+        bias[:, g * 128 : (g + 1) * 128] = jnp.where((lane & 63) < limit, 0.0, NEG)
+
+    pool_ready()
     lane8 = iota((8, 128), 1)
+
+    some = n_heads // 2
+
+    def back(d, i, target):
+        src, dst = (ml_out, ml_in) if i == 0 else (u_out, u_in)
+        src, dst = src.at[d], dst.at[d]
+        if i > 0:
+            src, dst = src.at[i - 1], dst.at[i - 1]
+        return pltpu.make_async_remote_copy(
+            src_ref=src, dst_ref=dst,
+            send_sem=usend_sem.at[d, i], recv_sem=urecv_sem.at[d, i],
+            device_id={"dp": target}, device_id_type=MESH,
+        )
 
     def far_terms(d, wuv_copy):
         ask(d, 2, plan.at[0], plan_in).wait_recv()
         c_sm = pltpu.make_async_copy(plan_in.at[d], plan_sm.at[d], sm_sem.at[d])
         c_sm.start()
         ask(d, 0, qn, qn_in).wait_recv()
-        ask(d, 1, qr, qr_in).wait_recv()
-        q_rope = qr_in[d]
         for h in range(n_heads):
             far = dot(qn_in[d, :, h * NOPE : (h + 1) * NOPE], wuk[h])
             at = pl.ds(h, reqs, stride=n_heads)
             for j in range(wide):
                 q_far[j, at, :] = far[:, j * 128 : (j + 1) * 128]
-            q_far[wide, at, :] = doubled_rope(q_rope, h)
+        ask(d, 1, qr, qr_in).wait_recv()
+        q_rope = qr_in[d]
+        for h in range(n_heads):
+            q_far[wide, pl.ds(h, reqs, stride=n_heads), :] = doubled_rope(q_rope, h)
         c_sm.wait()
 
         def held(pair):
@@ -248,7 +300,12 @@
             k_lat = jnp.concatenate([lat[slot] for slot, _ in found], axis=0)
             k_rope = jnp.concatenate([keys[slot] for slot, _ in found], axis=0)
             q_lat = jnp.concatenate([q_far[j, at, :] for j in range(wide)], axis=1).astype(BF16)
-            s = dot_t(q_lat, k_lat) + dot_t(q_far[wide, at, :].astype(BF16), k_rope)
+            q_rope = q_far[wide, at, :].astype(BF16)
+            if pair % 2:
+                s = dot_t(k_lat, q_lat) + dot_t(k_rope, q_rope)
+                s = jnp.concatenate([s[0:128].T, s[128:256].T], axis=1)
+            else:
+                s = dot_t(q_lat, k_lat) + dot_t(q_rope, k_rope)
             blocks = []
             for e in range(2):
                 limit = jnp.where(lane8 < 64, found[2 * e][1], found[2 * e + 1][1])
@@ -285,68 +342,89 @@
             if pair >= GROUP:
                 far_values(pair - GROUP, waiting.pop(pair - GROUP))
 
+        backs = []
+
+        def send_back(i):
+            copy = back(d, i, jnp.where(d == 0, nxt, prv))
+            copy.start()
+            backs.append(copy)
+
         if wuv_copy is not None:
-            wuv_copy.wait()
+
+            @pl.when(me == relay)
+            def _():
+                pl.semaphore_wait(gate_sem, 1)
+                for i in (2, 0, 1):
+                    to_relay(i).wait_recv()
+                    from_relay(i).start()
+
         pack = jnp.zeros((reqs, 128), F32)
         for h in range(n_heads):
             at = pl.ds(h, reqs, stride=n_heads)
-            o = jnp.concatenate([o_far[j, at, :] for j in range(wide)], axis=1)
-            u_out[d, :, h * VDIM : (h + 1) * VDIM] = dot(o.astype(BF16), wuv[h]).astype(BF16)
             pack = jnp.where(lane == h, m_far[at, :], pack)
             pack = jnp.where(lane == n_heads + h, l_far[at, :], pack)
         ml_out[d] = pack
-        backs = []
-        for i, (src, dst) in enumerate(((ml_out, ml_in), (u_out, u_in))):
-            copy = pltpu.make_async_remote_copy(
-                src_ref=src.at[d], dst_ref=dst.at[d],
-                send_sem=usend_sem.at[d, i], recv_sem=urecv_sem.at[d, i],
-                device_id={"dp": jnp.where(d == 0, nxt, prv)}, device_id_type=MESH,
+        send_back(0)
+        if wuv_copy is not None:
+            wuv_copy.wait()
+        for h in range(n_heads):
+            at = pl.ds(h, reqs, stride=n_heads)
+            o = jnp.concatenate([o_far[j, at, :] for j in range(wide)], axis=1)
+            u = dot(o.astype(BF16), wuv[h]).astype(BF16)
+            u_out[d, h // some, :, (h % some) * VDIM : (h % some + 1) * VDIM] = u
+            if h % some == some - 1:
+                send_back(1 + h // some)
+        return backs
+
+    backs = far_terms(near, c_wuv)
+    pl.when(me == 0)(own_scores)
+
+    backs += far_terms(1 - near, None)
+
+    pl.when(me != 0)(own_scores)
+
+
+    top = jnp.max(peaks[...], axis=1, keepdims=True)
+    span = 16 * PAGE
+    steps = slots // 16
+    parts_v = []
+    for i in range(steps + 1):
+        if i < steps:
+            base = top if i < 2 else top + parts_v[i - 2][:, 0:128] * 0.0
+            for h in range(n_heads):
+                mine = slice(h * reqs, (h + 1) * reqs)
+                total = None if i == 0 else totals[mine, :]
+                for j in range(span // 128):
+                    at = i * span + j * 128
+                    w = jnp.exp2((scores[mine, at : at + 128] - base[mine]) * SCALE2)
+                    total = w if total is None else total + w
+                    probs[mine, at : at + 128] = w.astype(BF16)
+                totals[mine, :] = total
+        if i > 0:
+            k = i - 1
+            part = dot(
+                probs[:, k * span : (k + 1) * span],
+                lat[k * 16 : (k + 1) * 16].reshape(span, latent),
             )
-            copy.start()
-            backs.append(copy)
-        return backs
-
-    backs = far_terms(near, c_wuv)
-
-    backs += far_terms(1 - near, None)
-
-    pl.when(me > 1)(own_scores)
-
-
-    top = jnp.max(peaks[...], axis=1, keepdims=True)
-    total = jnp.zeros((rows, 128), F32)
-    span = 16 * PAGE
-    for i in range(slots // 16):
-        for j in range(span // 128):
-            at = i * span + j * 128
-            w = jnp.exp2((scores[:, at : at + 128] - top) * SCALE2)
-            total = total + w
-            probs[:, at : at + 128] = w.astype(BF16)
-        part = dot(
-            probs[:, i * span : (i + 1) * span], lat[i * 16 : (i + 1) * 16].reshape(span, latent)
-        )
-        if i == 0:
-            acc[...] = part
-        else:
-            acc[...] += part
-    total = jnp.sum(total, axis=1, keepdims=True)
+            parts_v.append(part)
+            if k == 0:
+                acc[:, 0:latent] = part
+            else:
+                acc[:, 0:latent] += part
+    total = jnp.sum(totals[...], axis=1, keepdims=True)
 
     own_u = []
     m_own = jnp.zeros((reqs, 128), F32)
     l_own = jnp.zeros((reqs, 128), F32)
     for h in range(n_heads):
         mine = slice(h * reqs, (h + 1) * reqs)
-        own_u.append(dot(acc[mine, :].astype(BF16), wuv[h]))
+        own_u.append(dot(acc[mine, 0:latent].astype(BF16), wuv[h]))
         m_own = jnp.where(lane == h, top[mine], m_own)
         l_own = jnp.where(lane == h, total[mine], l_own)
 
     for d in range(2):
-        for i, (src, dst) in enumerate(((ml_out, ml_in), (u_out, u_in))):
-            pltpu.make_async_remote_copy(
-                src_ref=src.at[d], dst_ref=dst.at[d],
-                send_sem=usend_sem.at[d, i], recv_sem=urecv_sem.at[d, i],
-                device_id={"dp": nxt}, device_id_type=MESH,
-            ).wait_recv()
+        for i in range(3):
+            back(d, i, nxt).wait_recv()
 
     for copy in c_wo:
         copy.wait()
@@ -360,7 +438,10 @@
     fs = [f * share for f in fs]
     for h in range(n_heads):
         at = slice(h * VDIM, (h + 1) * VDIM)
-        us = [own_u[h], u_in[0, :, at].astype(F32), u_in[1, :, at].astype(F32)]
+        us = [own_u[h]] + [
+            u_in[d, h // some, :, (h % some) * VDIM : (h % some + 1) * VDIM].astype(F32)
+            for d in range(2)
+        ]
         gs = [jnp.broadcast_to(f[:, h : h + 1], (reqs, VDIM)) for f in fs]
         heads_out[:, at] = (gs[0] * us[0] + gs[1] * us[1] + gs[2] * us[2]).astype(BF16)
 
@@ -381,6 +462,11 @@
         out_ref[:, p * piece : (p + 1) * piece] = (mine[p] + y_in[p].astype(F32)).astype(BF16)
     for copy in asks + backs + sends:
         copy.wait_send()
+
+    @pl.when(me == relay)
+    def _():
+        for i in range(3):
+            from_relay(i).wait_send()
 
 def shards(
     n_dp, q_nope, q_rope, lengths, page_table, lend_counts, latent_pages, rope_pages, w_uk, w_uv, w_o
@@ -394,7 +480,7 @@
     vmem = pltpu.VMEM
     dma = pltpu.SemaphoreType.DMA
     return pl.pallas_call(
-        functools.partial(kernel, n_dp),
+        functools.partial(kernel, n_dp, RELAY if n_dp > RELAY + 1 else n_dp // 2),
         out_shape=jax.ShapeDtypeStruct((reqs, half), BF16),
         in_specs=[pl.BlockSpec(memory_space=pltpu.HBM)] * 10,
         out_specs=pl.BlockSpec(memory_space=vmem),
@@ -413,32 +499,39 @@
             vmem((2, *q_nope.shape), BF16),
             vmem((2, *q_rope.shape), BF16),
             vmem((2, 8, 128), jnp.int32),
+            vmem(q_nope.shape, BF16),
+            vmem(q_rope.shape, BF16),
+            vmem((8, 128), jnp.int32),
             pltpu.SMEM((2, 8, 128), jnp.int32),
             vmem((512, 256), BF16),
             vmem((slots, PAGE, 128), BF16),
             vmem((rows, latent + 128), BF16),
             vmem((reqs, tokens), F32),
-            vmem((rows, tokens), F32),
+            vmem((rows, tokens + 128), F32),
             vmem((rows, 128), F32),
-            vmem((rows, tokens), BF16),
-            vmem((rows, latent), F32),
+            vmem((rows, 128), F32),
+            vmem((rows, tokens + 128), BF16),
+            vmem((rows, latent + 128), F32),
             vmem((latent // 128 + 1, rows, 128), F32),
             vmem((latent // 128, rows, 128), F32),
             vmem((rows, 128), F32),
             vmem((rows, 128), F32),
-            vmem((2, reqs, n_heads * VDIM), BF16),
+            vmem((2, 2, reqs, n_heads // 2 * VDIM), BF16),
             vmem((2, reqs, 128), F32),
-            vmem((2, reqs, n_heads * VDIM), BF16),
+            vmem((2, 2, reqs, n_heads // 2 * VDIM), BF16),
             vmem((2, reqs, 128), F32),
             vmem((reqs, n_heads * VDIM), BF16),
             vmem((PARTS, reqs, half // PARTS), BF16),
             vmem((PARTS, reqs, half // PARTS), BF16),
-            dma((11 + 2 * PARTS,)),
+            dma((8 + 2 * PARTS + POOL_COPIES,)),
             dma((2,)),
+            pltpu.SemaphoreType.REGULAR,
+            dma((3,)),
+            dma((3,)),
             dma((2, 3)),
             dma((2, 3)),
-            dma((2, 2)),
-            dma((2, 2)),
+            dma((2, 3)),
+            dma((2, 3)),
             dma((PARTS,)),
             dma((PARTS,)),
         ],

time: 27 us -> 24.7 us (0.915)
  Pallas kernels: 26.2 us -> 23.9 us
    pallas_call x1, Pallas kernels: 26.2 us -> 23.9 us  [shards(): pl.pallas_call(functools.partial(kernel, n_dp, RELAY if n_dp > RELAY + 1...]
where the time goes in v3:
time: 24.7 us; the launch traced here: 24.6 us
  Pallas kernels  23.9 us (97%)
  local copies, waits for them, and re-layouts  0.63 us (3%)
    pallas_call x1, Pallas kernels, shards(): pl.pallas_call(functools.partial(kernel, n_dp, RELAY if n_dp > RELAY + 1...  23.9 us
    unnamed x1, local copies, waits for them, and re-layouts  0.63 us

profile of v3, /device:TPU:0, one launch (start us, length us, event | category | flops | bytes accessed | tf_op | source)
XLA Modules:
  0.0 24.6 jit_solution(7759691020032080576)
XLA Ops:
  0.0 23.9 %latent_step.1 = bf16[32,1024]{1,0:T(8,128)(2,1)S(1)} custom-call(bf16[32,1024]{1,0:T(8,128)(2,1)} %qn_hbm.1, bf16[32,512]{1,0:T(8,128)(2,1)} %qr_hbm.1, s32[8,32]{1,0:T(8,128)} %bitcast.3, s32[2,32]{1,0:T(2,128)} %bitcast.4, s32[1,32]{1,0:T(1,128)} %bitcast.5, bf16[96,64,512]{2,1,0:T(8,128)(2,1)} %lat_hbm.1, bf16[96,4096]{1,0:T(8,128)(2,1)} %rope_hbm.1, ...), custom_call_target="tpu_custom_call" | custom-call | tf_op jit(solution)/shard_map/latent_step/pallas_call | solution.py:482
  24.0 0.6 %copy.12 = bf16[32,1024]{1,0:T(8,128)(2,1)} copy(bf16[32,1024]{1,0:T(8,128)(2,1)S(1)} %latent_step.1) | data formatting | bytes 131072

commit v4 on v3

--- a/solution.py
+++ b/solution.py
@@ -100,6 +100,11 @@
         for i in range(POOL_COPIES)
     ]
 
+    @pl.when(me == last)
+    def _():
+        pl.semaphore_wait(barrier, 4)
+        pl.semaphore_signal(gate_sem, inc=1, device_id={"dp": relay}, device_id_type=MESH)
+
     out_row = iota((512, 256), 0)
     in_row = iota((512, 256), 1)
     hit = ((out_row >> 5) == (in_row & 15)) & (((out_row & 31) >> 1) == (in_row >> 4))
@@ -153,18 +158,15 @@
     c_qn.wait()
     c_qr.wait()
 
-    def pool_ready():
-        c_wuk.wait()
-        for copy in c_lat:
-            copy.wait()
-
-    def own_scores():
+    def own_queries():
         for h in range(n_heads):
             mine = pl.ds(h * reqs, reqs)
             q_own[mine, 0:latent] = dot(qn[:, h * NOPE : (h + 1) * NOPE], wuk[h]).astype(BF16)
             q_own[mine, latent : latent + 128] = doubled_rope(qr, h).astype(BF16)
-        top = None
-        for i in range(slots // 4):
+
+    def own_scores(begin, end):
+        top = None if begin == 0 else peaks[...]
+        for i in range(begin, end):
             at = i * 4 * PAGE
             s = dot_t(q_own[:, 0:latent], lat[i * 4 : i * 4 + 4].reshape(256, latent))
             s = s + dot_t(
@@ -177,10 +179,40 @@
             top = peak if top is None else jnp.maximum(top, peak)
         peaks[...] = top
 
-    @pl.when(me == last)
-    def _():
-        pl.semaphore_wait(barrier, 4)
-        pl.semaphore_signal(gate_sem, inc=1, device_id={"dp": relay}, device_id_type=MESH)
+    def own_values():
+        top = jnp.max(peaks[...], axis=1, keepdims=True)
+        span = 16 * PAGE
+        steps = slots // 16
+        parts_v = []
+        for i in range(steps + 1):
+            if i < steps:
+                base = top if i < 2 else top + parts_v[i - 2][:, 0:128] * 0.0
+                for h in range(n_heads):
+                    mine = slice(h * reqs, (h + 1) * reqs)
+                    total = None if i == 0 else totals[mine, :]
+                    for j in range(span // 128):
+                        at = i * span + j * 128
+                        w = jnp.exp2((scores[mine, at : at + 128] - base[mine]) * SCALE2)
+                        total = w if total is None else total + w
+                        probs[mine, at : at + 128] = w.astype(BF16)
+                    totals[mine, :] = total
+            if i > 0:
+                k = i - 1
+                part = dot(
+                    probs[:, k * span : (k + 1) * span],
+                    lat[k * 16 : (k + 1) * 16].reshape(span, latent),
+                )
+                parts_v.append(part)
+                if k == 0:
+                    acc[:, 0:latent] = part
+                else:
+                    acc[:, 0:latent] += part
+
+    def own_rest():
+        own_scores(early, slots // 4)
+        own_values()
+
+    early = (3 * (slots // POOL_COPIES)) // 4
 
     pl.when(me != last)(lambda: pl.semaphore_wait(barrier, 3))
 
@@ -216,13 +248,12 @@
         for i in (2, 0, 1):
             to_relay(i).start()
 
-    @pl.when(me != 0)
-    def _():
-        for copy in asks[:3]:
+    def start_asks(d):
+        for copy in asks[3 * d : 3 * d + 3]:
             copy.start()
 
-    for copy in asks[3:]:
-        copy.start()
+    pl.when((me != 0) & (me != relay + 1))(lambda: start_asks(0))
+    pl.when(me != relay - 2)(lambda: start_asks(1))
     c_wuv = local(wuv_hbm, wuv, 7)
     c_wo = [
         local(
@@ -255,7 +286,15 @@
         limit = jnp.where(lane < 64, even, odd)
         bias[:, g * 128 : (g + 1) * 128] = jnp.where((lane & 63) < limit, 0.0, NEG)
 
-    pool_ready()
+    c_wuk.wait()
+    for copy in c_lat[:3]:
+        copy.wait()
+    own_queries()
+    own_scores(0, early)
+    pl.when(me == relay + 1)(lambda: start_asks(0))
+    pl.when(me == relay - 2)(lambda: start_asks(1))
+    for copy in c_lat[3:]:
+        copy.wait()
     lane8 = iota((8, 128), 1)
 
     some = n_heads // 2
@@ -349,15 +388,6 @@
             copy.start()
             backs.append(copy)
 
-        if wuv_copy is not None:
-
-            @pl.when(me == relay)
-            def _():
-                pl.semaphore_wait(gate_sem, 1)
-                for i in (2, 0, 1):
-                    to_relay(i).wait_recv()
-                    from_relay(i).start()
-
         pack = jnp.zeros((reqs, 128), F32)
         for h in range(n_heads):
             at = pl.ds(h, reqs, stride=n_heads)
@@ -376,41 +406,21 @@
                 send_back(1 + h // some)
         return backs
 
+    @pl.when(me == relay)
+    def _():
+        pl.semaphore_wait(gate_sem, 1)
+        for i in (2, 0, 1):
+            to_relay(i).wait_recv()
+            from_relay(i).start()
+
     backs = far_terms(near, c_wuv)
-    pl.when(me == 0)(own_scores)
+    pl.when(me == 0)(own_rest)
 
     backs += far_terms(1 - near, None)
 
-    pl.when(me != 0)(own_scores)
-
+    pl.when(me != 0)(own_rest)
 
     top = jnp.max(peaks[...], axis=1, keepdims=True)
-    span = 16 * PAGE
-    steps = slots // 16
-    parts_v = []
-    for i in range(steps + 1):
-        if i < steps:
-            base = top if i < 2 else top + parts_v[i - 2][:, 0:128] * 0.0
-            for h in range(n_heads):
-                mine = slice(h * reqs, (h + 1) * reqs)
-                total = None if i == 0 else totals[mine, :]
-                for j in range(span // 128):
-                    at = i * span + j * 128
-                    w = jnp.exp2((scores[mine, at : at + 128] - base[mine]) * SCALE2)
-                    total = w if total is None else total + w
-                    probs[mine, at : at + 128] = w.astype(BF16)
-                totals[mine, :] = total
-        if i > 0:
-            k = i - 1
-            part = dot(
-                probs[:, k * span : (k + 1) * span],
-                lat[k * 16 : (k + 1) * 16].reshape(span, latent),
-            )
-            parts_v.append(part)
-            if k == 0:
-                acc[:, 0:latent] = part
-            else:
-                acc[:, 0:latent] += part
     total = jnp.sum(totals[...], axis=1, keepdims=True)
 
     own_u = []

time: 24.7 us -> 24 us (0.972)
  Pallas kernels: 23.9 us -> 23.1 us
    pallas_call x1, Pallas kernels: 23.9 us -> 23.1 us  [shards(): pl.pallas_call(functools.partial(kernel, n_dp, RELAY if n_dp > RELAY + 1...]
where the time goes in v4:
time: 24 us; the launch traced here: 23.7 us
  Pallas kernels  23.1 us (96%)
  local copies, waits for them, and re-layouts  0.63 us (3%)
    pallas_call x1, Pallas kernels, shards(): pl.pallas_call(functools.partial(kernel, n_dp, RELAY if n_dp > RELAY + 1...  23.1 us
    unnamed x1, local copies, waits for them, and re-layouts  0.63 us

profile of v4, /device:TPU:0, one launch (start us, length us, event | category | flops | bytes accessed | tf_op | source)
XLA Modules:
  0.0 23.7 jit_solution(6744137986018833630)
XLA Ops:
  0.0 23.1 %latent_step.1 = bf16[32,1024]{1,0:T(8,128)(2,1)S(1)} custom-call(bf16[32,1024]{1,0:T(8,128)(2,1)} %qn_hbm.1, bf16[32,512]{1,0:T(8,128)(2,1)} %qr_hbm.1, s32[8,32]{1,0:T(8,128)} %bitcast.3, s32[2,32]{1,0:T(2,128)} %bitcast.4, s32[1,32]{1,0:T(1,128)} %bitcast.5, bf16[96,64,512]{2,1,0:T(8,128)(2,1)} %lat_hbm.1, bf16[96,4096]{1,0:T(8,128)(2,1)} %rope_hbm.1, ...), custom_call_target="tpu_custom_call" | custom-call | tf_op jit(solution)/shard_map/latent_step/pallas_call | solution.py:492
  23.1 0.6 %copy.12 = bf16[32,1024]{1,0:T(8,128)(2,1)} copy(bf16[32,1024]{1,0:T(8,128)(2,1)S(1)} %latent_step.1) | data formatting | bytes 131072

commit v5 on v4

--- a/solution.py
+++ b/solution.py
@@ -137,6 +137,27 @@
             packed = jnp.where(row8 == j, slot, packed)
             packed = jnp.where(row8 == LEND + j, live, packed)
         plan[d, :, 0:reqs] = packed
+
+    lane = iota((reqs, 128), 1)
+    facts = jnp.concatenate([pages, first, length], axis=0).astype(F32)
+    facts = jnp.concatenate([facts, jnp.zeros((24, 128 - reqs), F32)], axis=1)
+    facts = jnp.concatenate([facts, jnp.zeros((104, 128), F32)], axis=0)
+    facts = jnp.transpose(facts)[0:reqs].astype(jnp.int32)
+
+    def column(i):
+        return jnp.broadcast_to(facts[:, i : i + 1], (reqs, 128))
+
+    first = column(8)
+    length = column(16)
+    count = jnp.zeros((reqs, 128), jnp.int32)
+    for k in range(MAXP):
+        live = jnp.clip(length - k * PAGE, 0, PAGE)
+        count = count + jnp.where((lane == column(k)) & (first > k), live, 0)
+    for g in range(slots // 2):
+        even = jnp.broadcast_to(count[:, 2 * g : 2 * g + 1], (reqs, 128))
+        odd = jnp.broadcast_to(count[:, 2 * g + 1 : 2 * g + 2], (reqs, 128))
+        limit = jnp.where(lane < 64, even, odd)
+        bias[:, g * 128 : (g + 1) * 128] = jnp.where((lane & 63) < limit, 0.0, NEG)
 
     c_rope.wait()
     row_odd = (iota((512, 128), 0) & 1) == 1
@@ -229,24 +250,32 @@
         asks.append(ask(d, 0, qn, qn_in))
         asks.append(ask(d, 1, qr, qr_in))
 
-    def to_relay(i):
+    low = reqs // 2
+    relayed = ((2, 0), (0, 0), (0, 1), (1, 0), (1, 1))
+
+    def part(ref, i, e):
+        return ref if i == 2 else ref.at[pl.ds(e * low, low)]
+
+    def to_relay(i, e):
         src, dst = [(qn, qn_by), (qr, qr_by), (plan.at[0], plan_by)][i]
         return pltpu.make_async_remote_copy(
-            src_ref=src, dst_ref=dst, send_sem=qsend_sem.at[0, i], recv_sem=byrecv_sem.at[i],
+            src_ref=part(src, i, e), dst_ref=part(dst, i, e),
+            send_sem=qsend_sem.at[0, i], recv_sem=byrecv_sem.at[i, e],
             device_id={"dp": relay}, device_id_type=MESH,
         )
 
-    def from_relay(i):
+    def from_relay(i, e):
         src, dst = [(qn_by, qn_in), (qr_by, qr_in), (plan_by, plan_in)][i]
         return pltpu.make_async_remote_copy(
-            src_ref=src, dst_ref=dst.at[0], send_sem=bysend_sem.at[i], recv_sem=qrecv_sem.at[0, i],
+            src_ref=part(src, i, e), dst_ref=part(dst.at[0], i, e),
+            send_sem=bysend_sem.at[i, e], recv_sem=qrecv_sem.at[0, i],
             device_id={"dp": last}, device_id_type=MESH,
         )
 
     @pl.when(me == 0)
     def _():
-        for i in (2, 0, 1):
-            to_relay(i).start()
+        for i, e in relayed:
+            to_relay(i, e).start()
 
     def start_asks(d):
         for copy in asks[3 * d : 3 * d + 3]:
@@ -264,27 +293,6 @@
         local(wo_hbm.at[:, pl.ds(side * half + p * piece, piece)], wo.at[parts + p], 8 + parts + p)
         for p in range(parts)
     ]
-
-    lane = iota((reqs, 128), 1)
-    facts = jnp.concatenate([pages, first, length], axis=0).astype(F32)
-    facts = jnp.concatenate([facts, jnp.zeros((24, 128 - reqs), F32)], axis=1)
-    facts = jnp.concatenate([facts, jnp.zeros((104, 128), F32)], axis=0)
-    facts = jnp.transpose(facts)[0:reqs].astype(jnp.int32)
-
-    def column(i):
-        return jnp.broadcast_to(facts[:, i : i + 1], (reqs, 128))
-
-    first = column(8)
-    length = column(16)
-    count = jnp.zeros((reqs, 128), jnp.int32)
-    for k in range(MAXP):
-        live = jnp.clip(length - k * PAGE, 0, PAGE)
-        count = count + jnp.where((lane == column(k)) & (first > k), live, 0)
-    for g in range(slots // 2):
-        even = jnp.broadcast_to(count[:, 2 * g : 2 * g + 1], (reqs, 128))
-        odd = jnp.broadcast_to(count[:, 2 * g + 1 : 2 * g + 2], (reqs, 128))
-        limit = jnp.where(lane < 64, even, odd)
-        bias[:, g * 128 : (g + 1) * 128] = jnp.where((lane & 63) < limit, 0.0, NEG)
 
     c_wuk.wait()
     for copy in c_lat[:3]:
@@ -409,9 +417,9 @@
     @pl.when(me == relay)
     def _():
         pl.semaphore_wait(gate_sem, 1)
-        for i in (2, 0, 1):
-            to_relay(i).wait_recv()
-            from_relay(i).start()
+        for i, e in relayed:
+            to_relay(i, e).wait_recv()
+            from_relay(i, e).start()
 
     backs = far_terms(near, c_wuv)
     pl.when(me == 0)(own_rest)
@@ -475,8 +483,8 @@
 
     @pl.when(me == relay)
     def _():
-        for i in range(3):
-            from_relay(i).wait_send()
+        for i, e in relayed:
+            from_relay(i, e).wait_send()
 
 def shards(
     n_dp, q_nope, q_rope, lengths, page_table, lend_counts, latent_pages, rope_pages, w_uk, w_uv, w_o
@@ -536,8 +544,8 @@
             dma((8 + 2 * PARTS + POOL_COPIES,)),
             dma((2,)),
             pltpu.SemaphoreType.REGULAR,
-            dma((3,)),
-            dma((3,)),
+            dma((3, 2)),
+            dma((3, 2)),
             dma((2, 3)),
             dma((2, 3)),
             dma((2, 3)),

time: 24 us -> 24.1 us (level)
  no operation moved by 1% of the time
where the time goes in v5:
time: 24.1 us; the launch traced here: 23.8 us
  Pallas kernels  23.2 us (96%)
  local copies, waits for them, and re-layouts  0.63 us (3%)
    pallas_call x1, Pallas kernels, shards(): pl.pallas_call(functools.partial(kernel, n_dp, RELAY if n_dp > RELAY + 1...  23.2 us
    unnamed x1, local copies, waits for them, and re-layouts  0.63 us

profile of v5, /device:TPU:0, one launch (start us, length us, event | category | flops | bytes accessed | tf_op | source)
XLA Modules:
  0.0 23.8 jit_solution(11086427132901277323)
XLA Ops:
  0.0 23.2 %latent_step.1 = bf16[32,1024]{1,0:T(8,128)(2,1)S(1)} custom-call(bf16[32,1024]{1,0:T(8,128)(2,1)} %qn_hbm.1, bf16[32,512]{1,0:T(8,128)(2,1)} %qr_hbm.1, s32[8,32]{1,0:T(8,128)} %bitcast.3, s32[2,32]{1,0:T(2,128)} %bitcast.4, s32[1,32]{1,0:T(1,128)} %bitcast.5, bf16[96,64,512]{2,1,0:T(8,128)(2,1)} %lat_hbm.1, bf16[96,4096]{1,0:T(8,128)(2,1)} %rope_hbm.1, ...), custom_call_target="tpu_custom_call" | custom-call | tf_op jit(solution)/shard_map/latent_step/pallas_call | solution.py:500
  23.2 0.6 %copy.12 = bf16[32,1024]{1,0:T(8,128)(2,1)} copy(bf16[32,1024]{1,0:T(8,128)(2,1)S(1)} %latent_step.1) | data formatting | bytes 131072
